TPU v7x, 32 devices: a whole 2x2x4 slice. The times are simulated.
32 devices in a mesh: fsdp: 4 (over z), context: 2 (over x), tensor: 4 (over y, core).
Axes of the slice: x: 2, y: 2, z: 4, core: 2. Of those that a mesh axis runs over, the one named last changes fastest.
Arguments:
- tokens: bfloat16 [8, 1024, 768], P('fsdp', 'context'), may hold values from -6 to 6
- cotangent: bfloat16 [8, 1024, 768], P('fsdp', 'context'), may hold values from -6 to 6
- segment_ids: int32 [8, 1024], P('fsdp', 'context'), may hold values from 0 to 15, never falling along the last dimension, each value on 1 to 512 neighbouring positions
- owner: int32 [4], replicated, may hold values from 0 to 1, as said below
- qkv_weight: float32 [768, 3, 768], P('fsdp', None, 'tensor'), may hold values from -0.21875 to 0.21875
- out_weight: float32 [768, 768], P('tensor', 'fsdp'), may hold values from -1.25 to 1.25
- gate_up_weight: float32 [768, 2, 3072], P('fsdp', None, 'tensor'), may hold values from -0.21875 to 0.21875
- down_weight: float32 [3072, 768], P('tensor', 'fsdp'), may hold values from -0.109375 to 0.109375
- norm_gains: float32 [2, 768], replicated, may hold values from 0.5 to 1.5
- norm_biases: float32 [2, 768], replicated, may hold values from -2 to 2
- qkv_moment: float32 [2, 768, 3, 768], P('context', 'fsdp', None, 'tensor'), may hold values from -32 to 32
- qkv_square: float32 [2, 768, 3, 768], P('context', 'fsdp', None, 'tensor'), may hold values from 1 to 10
- out_moment: float32 [2, 768, 768], P('context', 'tensor', 'fsdp'), may hold values from -32 to 32
- out_square: float32 [2, 768, 768], P('context', 'tensor', 'fsdp'), may hold values from 1 to 10
- gate_moment: float32 [2, 768, 2, 3072], P('context', 'fsdp', None, 'tensor'), may hold values from -32 to 32
- gate_square: float32 [2, 768, 2, 3072], P('context', 'fsdp', None, 'tensor'), may hold values from 1 to 10
- down_moment: float32 [2, 3072, 768], P('context', 'tensor', 'fsdp'), may hold values from -32 to 32
- down_square: float32 [2, 3072, 768], P('context', 'tensor', 'fsdp'), may hold values from 1 to 10
- norm_moment: float32 [4, 768], replicated, may hold values from -32 to 32
- norm_square: float32 [4, 768], replicated, may hold values from 1 to 10
Outputs:
- layer_out: bfloat16 [8, 1024, 768], P('fsdp', ('context', 'tensor'))
- input_grad: float32 [8, 1024, 768], P('fsdp', ('context', 'tensor'))
- qkv_grad: float32 [768, 3, 768], P('fsdp', None, 'tensor')
- out_grad: float32 [768, 768], P('tensor', 'fsdp')
- gate_up_grad: float32 [768, 2, 3072], P('fsdp', None, 'tensor')
- down_grad: float32 [3072, 768], P('tensor', 'fsdp')
- norm_grad: float32 [4, 768], replicated
- qkv_state: float32 [2, 768, 3, 768], P(None, 'fsdp', None, 'tensor')
- out_state: float32 [2, 768, 768], P(None, 'tensor', 'fsdp')
- gate_up_state: float32 [2, 768, 2, 3072], P(None, 'fsdp', None, 'tensor')
- down_state: float32 [2, 3072, 768], P(None, 'tensor', 'fsdp')
- norm_state: float32 [2, 4, 768], replicated
- weight_updates: float32 [4, 4, 590016], P('fsdp', 'tensor')
Inputs may be any that keep to these rules, and one draw needn't show every extreme that they name: `segment_ids`: within each sequence the ids never fall; each of 0 to 15 names one document of 1 to 512 tokens, and one document has exactly 512. Some matrix has owner 0 and some other has owner 2 - 1.
All inputs are finite; a program needn't handle non-finite values.
Results may differ from a plain program's by a relative error of at most 0.03.
Values may be sent and summed in bfloat16 or wider, within the bound.
A program may use at most 192 MiB of HBM per device.

v0:
```python
import jax
import jax.numpy as jnp
from jax import lax
from jax.sharding import PartitionSpec as P

HD = 64


NEGATIVE = -1e30
EPSILON = 1e-05
ROPE_BASE = 1000.0
BETA_ONE = 0.9
BETA_TWO = 0.999
ADAM_EPS = 1e-08
ADAM_STEP = 3.0
RATE = 0.03
DECAY = 0.1


def from_root(block, axis, owner):
    block = jnp.where(lax.axis_index(axis) == owner, block, jnp.zeros_like(block))
    return lax.psum(block, axis)


def rotary_tables(positions, head_size):
    frequency = jnp.power(
        jnp.float32(ROPE_BASE), -jnp.arange(0, head_size, 2, dtype=jnp.float32) / head_size
    )
    angles = positions[:, None] * frequency[None, :]
    return (jnp.cos(angles), jnp.sin(angles))


def rotate(vectors, cosine, sine_rows):
    half_size = vectors.shape[-1] // 2
    first_half = vectors[..., :half_size]
    second_half = vectors[..., half_size:]
    cosine = cosine[:, None, :]
    sine_rows = sine_rows[:, None, :]
    return jnp.concatenate(
        [
            first_half * cosine - second_half * sine_rows,
            second_half * cosine + first_half * sine_rows,
        ],
        axis=-1,
    )


def normalize(values, gain_row, bias_row):
    center = values - jnp.mean(values, axis=-1, keepdims=True)
    variance = jnp.mean(center * center, axis=-1, keepdims=True)
    inverse_std = lax.rsqrt(variance + EPSILON)
    normed = center * inverse_std
    return (normed * gain_row + bias_row, normed, inverse_std)


def norm_back(gradient, normed, inverse_std, gain_row):
    scaled = gradient * gain_row
    first_mean = jnp.mean(scaled, axis=-1, keepdims=True)
    second_mean = jnp.mean(scaled * normed, axis=-1, keepdims=True)
    return inverse_std * (scaled - first_mean - normed * second_mean)


def rows_of(values, start, count):
    return lax.dynamic_slice_in_dim(values, start, count, 0)


def key_slice(pair_rows, key_ids, first_row, key_block, heads_here):
    pair_block = lax.dynamic_slice_in_dim(pair_rows, first_row, key_block, 0)
    half_cols = pair_block.shape[1] // 2
    key_rows = pair_block[:, :half_cols].reshape(key_block, heads_here, -1)
    value_rows = pair_block[:, half_cols:].reshape(key_block, heads_here, -1)
    block_ids = lax.dynamic_slice_in_dim(key_ids, first_row, key_block, 0)
    return (key_rows, value_rows, block_ids)


def block_scores(query_part, query_ids, key_rows, block_ids, scale):
    scores = (
        jnp.einsum("qhd,khd->hqk", query_part, key_rows, preferred_element_type=jnp.float32) * scale
    )
    return jnp.where(query_ids[None, :, None] == block_ids[None, None, :], scores, NEGATIVE)


def touches(query_ids, block_ids):
    return jnp.logical_and(
        jnp.max(block_ids) >= jnp.min(query_ids), jnp.min(block_ids) <= jnp.max(query_ids)
    )


def attend_forward(query_part, query_ids, pair_rows, key_ids, key_block, key_count, scale):
    heads_here = query_part.shape[1]
    query_rows = query_part.shape[0]

    def one_pass(block_index, state_all):
        key_rows, value_rows, block_ids = key_slice(
            pair_rows, key_ids, block_index * key_block, key_block, heads_here
        )

        def one_visit(inner_state):
            running, row_total, summed = inner_state
            scores = block_scores(query_part, query_ids, key_rows, block_ids, scale)
            newest = jnp.maximum(running, jnp.max(scores, axis=-1))
            shrink = jnp.exp(running - newest)
            weights = jnp.exp(scores - newest[..., None])
            row_total = row_total * shrink + jnp.sum(weights, axis=-1)
            summed = summed * jnp.transpose(shrink)[:, :, None] + jnp.einsum(
                "hqk,khd->qhd",
                weights.astype(jnp.bfloat16),
                value_rows,
                preferred_element_type=jnp.float32,
            )
            return (newest, row_total, summed)

        return lax.cond(
            touches(query_ids, block_ids), one_visit, lambda inner_state: inner_state, state_all
        )

    start_state = (
        jnp.full((heads_here, query_rows), NEGATIVE, jnp.float32),
        jnp.zeros((heads_here, query_rows), jnp.float32),
        jnp.zeros(query_part.shape, jnp.float32),
    )
    running, row_total, summed = lax.fori_loop(0, key_count, one_pass, start_state)
    attended = summed / jnp.transpose(row_total)[:, :, None]
    totals = running + jnp.log(row_total)
    return (attended, totals)


def attend_backward(
    query_part,
    query_ids,
    pair_rows,
    key_ids,
    totals,
    row_delta,
    grad_part,
    key_block,
    key_count,
    scale,
):
    heads_here = query_part.shape[1]

    def grad_step(block_index, state_pair):
        first_row = block_index * key_block
        key_rows, value_rows, block_ids = key_slice(
            pair_rows, key_ids, first_row, key_block, heads_here
        )

        def grad_visit(inner_pair):
            grad_query, grad_pairs = inner_pair
            scores = block_scores(query_part, query_ids, key_rows, block_ids, scale)
            probability = jnp.exp(scores - totals[..., None])
            grad_probs = jnp.einsum(
                "qhd,khd->hqk", grad_part, value_rows, preferred_element_type=jnp.float32
            )
            grad_scores = (probability * (grad_probs - row_delta[..., None])).astype(jnp.bfloat16)
            grad_query = (
                grad_query
                + jnp.einsum(
                    "hqk,khd->qhd", grad_scores, key_rows, preferred_element_type=jnp.float32
                )
                * scale
            )
            grad_keys = (
                jnp.einsum(
                    "hqk,qhd->khd", grad_scores, query_part, preferred_element_type=jnp.float32
                )
                * scale
            )
            grad_values = jnp.einsum(
                "hqk,qhd->khd",
                probability.astype(jnp.bfloat16),
                grad_part,
                preferred_element_type=jnp.float32,
            )
            block_grad = jnp.concatenate(
                [grad_keys.reshape(key_block, -1), grad_values.reshape(key_block, -1)], axis=1
            )
            grad_pairs = lax.dynamic_update_slice_in_dim(grad_pairs, block_grad, first_row, 0)
            return (grad_query, grad_pairs)

        return lax.cond(
            touches(query_ids, block_ids), grad_visit, lambda inner_pair: inner_pair, state_pair
        )

    start_pair = (jnp.zeros(query_part.shape, jnp.float32), jnp.zeros(pair_rows.shape, jnp.float32))
    return lax.fori_loop(0, key_count, grad_step, start_pair)


def moment_pair(gradient, moment, square):
    moment_new = BETA_ONE * moment + (1.0 - BETA_ONE) * gradient
    square_new = BETA_TWO * square + (1.0 - BETA_TWO) * gradient * gradient
    return jnp.stack([moment_new, square_new])


def step_of(pair_new, master, decay_rate):
    corrected = pair_new[0] / (1.0 - BETA_ONE**ADAM_STEP)
    scaled = pair_new[1] / (1.0 - BETA_TWO**ADAM_STEP)
    return -RATE * (corrected / (jnp.sqrt(scaled) + ADAM_EPS) + decay_rate * master)


def owner_pair(stacked, root_index):
    return from_root(stacked.astype(jnp.bfloat16), "context", root_index).astype(stacked.dtype)


def shards(
    tokens,
    cotangent,
    segment_ids,
    owner,
    qkv_weight,
    out_weight,
    gate_up_weight,
    down_weight,
    norm_gains,
    norm_biases,
    qkv_moment,
    qkv_square,
    out_moment,
    out_square,
    gate_moment,
    gate_square,
    down_moment,
    down_square,
    norm_moment,
    norm_square,
):
    seqs_here, tok_here, model_width = tokens.shape
    row_count = seqs_here * tok_here
    head_cols = qkv_weight.shape[2]
    heads_here = head_cols // HD
    hidden_here = gate_up_weight.shape[2]
    context_size = lax.axis_size("context")
    tensor_size = lax.axis_size("tensor")
    fsdp_size = lax.axis_size("fsdp")
    tok_share = tok_here // tensor_size
    share_rows = tok_share * seqs_here
    share_start = lax.axis_index("tensor") * share_rows
    seq_length = tok_here * context_size
    key_block = min(512, seq_length)
    key_count = seq_length // key_block
    scale = HD ** (-0.5)
    masters = (qkv_weight, out_weight, gate_up_weight, down_weight)
    moment_pairs = (
        (qkv_moment, qkv_square),
        (out_moment, out_square),
        (gate_moment, gate_square),
        (down_moment, down_square),
    )
    low_weights = (
        qkv_weight.astype(jnp.bfloat16),
        out_weight.astype(jnp.bfloat16),
        gate_up_weight.astype(jnp.bfloat16),
        down_weight.astype(jnp.bfloat16),
    )
    qkv_full, out_full, gate_full, down_full = (
        lax.all_gather(low_weights[0], "fsdp", axis=0, tiled=True),
        lax.all_gather(low_weights[1], "fsdp", axis=1, tiled=True),
        lax.all_gather(low_weights[2], "fsdp", axis=0, tiled=True),
        lax.all_gather(low_weights[3], "fsdp", axis=1, tiled=True),
    )
    positions = (
        lax.axis_index("context") * tok_here + jnp.arange(tok_here, dtype=jnp.int32)
    ).astype(jnp.float32)
    cosine, sine_rows = rotary_tables(positions, HD)
    cosine = jnp.repeat(cosine, seqs_here, axis=0)
    sine_rows = jnp.repeat(sine_rows, seqs_here, axis=0)
    inputs = jnp.transpose(tokens, (1, 0, 2)).reshape(row_count, model_width)
    projected = jnp.dot(
        inputs, qkv_full.reshape(model_width, 3 * head_cols), preferred_element_type=jnp.float32
    )
    projected = projected.reshape(row_count, 3, heads_here, HD)
    queries = rotate(projected[:, 0], cosine, sine_rows).astype(jnp.bfloat16)
    key_local = rotate(projected[:, 1], cosine, sine_rows).astype(jnp.bfloat16)
    value_local = projected[:, 2].astype(jnp.bfloat16)
    pairs_local = jnp.concatenate(
        [key_local.reshape(row_count, head_cols), value_local.reshape(row_count, head_cols)], axis=1
    )
    pairs_local = jnp.transpose(pairs_local.reshape(tok_here, seqs_here, 2 * head_cols), (1, 0, 2))
    pairs_all, ids_all = (
        lax.all_gather(pairs_local, "context", axis=1, tiled=True),
        lax.all_gather(segment_ids, "context", axis=1, tiled=True),
    )
    query_seqs = jnp.transpose(queries.reshape(tok_here, seqs_here, heads_here, HD), (1, 0, 2, 3))

    def forward_one(packed):
        return attend_forward(
            packed[0], packed[1], packed[2], packed[3], key_block, key_count, scale
        )

    attended, totals = lax.map(forward_one, (query_seqs, segment_ids, pairs_all, ids_all))
    attended_low = (
        jnp.transpose(attended, (1, 0, 2, 3)).reshape(row_count, head_cols).astype(jnp.bfloat16)
    )
    attention_share = lax.psum_scatter(
        jnp.dot(
            rows_of(attended_low, jnp.int32(0), share_rows * lax.axis_size("tensor")),
            out_full,
            preferred_element_type=jnp.float32,
        ).astype(jnp.bfloat16),
        "tensor",
        scatter_dimension=0,
        tiled=True,
    ).astype(jnp.float32)
    input_share = rows_of(inputs, share_start, share_rows).astype(jnp.float32)
    normed_first, unit_first, inverse_first = normalize(
        input_share + attention_share, norm_gains[0], norm_biases[0]
    )
    normed_low = lax.all_gather(normed_first.astype(jnp.bfloat16), "tensor", axis=0, tiled=True)
    gate_up = jnp.dot(
        normed_low,
        gate_full.reshape(model_width, 2 * hidden_here),
        preferred_element_type=jnp.float32,
    )
    gate_up = gate_up.reshape(row_count, 2, hidden_here)
    gate_part = gate_up[:, 0]
    upward = gate_up[:, 1]
    hidden_low = (jax.nn.silu(gate_part) * upward).astype(jnp.bfloat16)
    ffn_share = lax.psum_scatter(
        jnp.dot(
            rows_of(hidden_low, jnp.int32(0), share_rows * lax.axis_size("tensor")),
            down_full,
            preferred_element_type=jnp.float32,
        ).astype(jnp.bfloat16),
        "tensor",
        scatter_dimension=0,
        tiled=True,
    ).astype(jnp.float32)
    layer_share, unit_second, inverse_second = normalize(
        normed_first + ffn_share, norm_gains[1], norm_biases[1]
    )
    grad_rows = jnp.transpose(cotangent, (1, 0, 2)).reshape(row_count, model_width)
    grad_out = rows_of(grad_rows, share_start, share_rows).astype(jnp.float32)
    gain_second = jnp.sum(grad_out * unit_second, axis=0)
    bias_second = jnp.sum(grad_out, axis=0)
    grad_z = norm_back(grad_out, unit_second, inverse_second, norm_gains[1])
    grad_z_low = lax.all_gather(grad_z.astype(jnp.bfloat16), "tensor", axis=0, tiled=True)
    down_term = jnp.einsum("rf,rd->fd", hidden_low, grad_z_low, preferred_element_type=jnp.float32)
    grad_hidden = jnp.einsum("rd,fd->rf", grad_z_low, down_full, preferred_element_type=jnp.float32)
    silu_product, silu_pull = jax.vjp(
        lambda gate_in, up_in: jax.nn.silu(gate_in) * up_in, gate_part, upward
    )
    grad_gate, grad_up = silu_pull(grad_hidden)
    grad_gate_up = jnp.stack([grad_gate, grad_up], axis=1).astype(jnp.bfloat16)
    gate_term = jnp.einsum(
        "rd,rgf->dgf", normed_low, grad_gate_up, preferred_element_type=jnp.float32
    )
    grad_normed = grad_z + lax.psum_scatter(
        jnp.einsum(
            "rgf,dgf->rd",
            rows_of(grad_gate_up, jnp.int32(0), share_rows * lax.axis_size("tensor")),
            gate_full,
            preferred_element_type=jnp.float32,
        ).astype(jnp.bfloat16),
        "tensor",
        scatter_dimension=0,
        tiled=True,
    ).astype(jnp.float32)
    gain_first = jnp.sum(grad_normed * unit_first, axis=0)
    bias_first = jnp.sum(grad_normed, axis=0)
    grad_pre = norm_back(grad_normed, unit_first, inverse_first, norm_gains[0])
    grad_pre_low = lax.all_gather(grad_pre.astype(jnp.bfloat16), "tensor", axis=0, tiled=True)
    out_term = jnp.einsum(
        "rc,rd->cd", attended_low, grad_pre_low, preferred_element_type=jnp.float32
    )
    grad_attended = jnp.einsum(
        "rd,cd->rc", grad_pre_low, out_full, preferred_element_type=jnp.float32
    ).astype(jnp.bfloat16)
    grad_seqs = jnp.transpose(
        grad_attended.reshape(tok_here, seqs_here, heads_here, HD), (1, 0, 2, 3)
    )
    row_delta = jnp.transpose(jnp.sum(grad_seqs.astype(jnp.float32) * attended, axis=-1), (0, 2, 1))

    def backward_one(packed):
        return attend_backward(
            packed[0],
            packed[1],
            packed[2],
            packed[3],
            packed[4],
            packed[5],
            packed[6],
            key_block,
            key_count,
            scale,
        )

    grad_queries, grad_pairs = lax.map(
        backward_one, (query_seqs, segment_ids, pairs_all, ids_all, totals, row_delta, grad_seqs)
    )
    grad_pairs_own = lax.psum_scatter(
        grad_pairs.astype(jnp.bfloat16), "context", scatter_dimension=1, tiled=True
    ).astype(jnp.float32)
    grad_pairs_own = jnp.transpose(grad_pairs_own, (1, 0, 2)).reshape(row_count, 2 * head_cols)
    grad_query_rows = jnp.transpose(grad_queries, (1, 0, 2, 3)).reshape(row_count, heads_here, HD)
    grad_query_raw = rotate(grad_query_rows, cosine, -sine_rows)
    grad_key_raw = rotate(
        grad_pairs_own[:, :head_cols].reshape(row_count, heads_here, HD), cosine, -sine_rows
    )
    grad_value_raw = grad_pairs_own[:, head_cols:].reshape(row_count, heads_here, HD)
    grad_projected = (
        jnp.stack([grad_query_raw, grad_key_raw, grad_value_raw], axis=1)
        .reshape(row_count, 3, head_cols)
        .astype(jnp.bfloat16)
    )
    qkv_term = jnp.einsum("rd,rtc->dtc", inputs, grad_projected, preferred_element_type=jnp.float32)
    input_grad = grad_pre + lax.psum_scatter(
        jnp.einsum(
            "rtc,dtc->rd",
            rows_of(grad_projected, jnp.int32(0), share_rows * lax.axis_size("tensor")),
            qkv_full,
            preferred_element_type=jnp.float32,
        ).astype(jnp.bfloat16),
        "tensor",
        scatter_dimension=0,
        tiled=True,
    ).astype(jnp.float32)
    grad_terms = (qkv_term, out_term, gate_term, down_term)
    grouped = (
        lax.psum_scatter(
            grad_terms[0].astype(jnp.bfloat16), "fsdp", scatter_dimension=0, tiled=True
        ).astype(jnp.float32),
        lax.psum_scatter(
            grad_terms[1].astype(jnp.bfloat16), "fsdp", scatter_dimension=1, tiled=True
        ).astype(jnp.float32),
        lax.psum_scatter(
            grad_terms[2].astype(jnp.bfloat16), "fsdp", scatter_dimension=0, tiled=True
        ).astype(jnp.float32),
        lax.psum_scatter(
            grad_terms[3].astype(jnp.bfloat16), "fsdp", scatter_dimension=1, tiled=True
        ).astype(jnp.float32),
    )
    weight_grads = (
        lax.psum(grouped[0].astype(jnp.bfloat16), "context").astype(jnp.float32),
        lax.psum(grouped[1].astype(jnp.bfloat16), "context").astype(jnp.float32),
        lax.psum(grouped[2].astype(jnp.bfloat16), "context").astype(jnp.float32),
        lax.psum(grouped[3].astype(jnp.bfloat16), "context").astype(jnp.float32),
    )
    norm_terms = jnp.stack([gain_first, gain_second, bias_first, bias_second])
    norm_grad = lax.psum(norm_terms, ("fsdp", "context", "tensor"))
    new_pairs = [
        owner_pair(
            moment_pair(
                weight_grads[matrix_index],
                moment_pairs[matrix_index][0][0],
                moment_pairs[matrix_index][1][0],
            ),
            owner[matrix_index],
        )
        for matrix_index in range(4)
    ]
    new_steps = [
        step_of(new_pairs[matrix_index], masters[matrix_index], DECAY) for matrix_index in range(4)
    ]
    norm_master = jnp.concatenate([norm_gains, norm_biases], axis=0)
    norm_state = moment_pair(norm_grad, norm_moment, norm_square)
    norm_step = step_of(norm_state, norm_master, 0.0).reshape(-1)
    norm_piece_size = norm_step.shape[0] // (fsdp_size * tensor_size)
    norm_start = (lax.axis_index("fsdp") * tensor_size + lax.axis_index("tensor")) * norm_piece_size
    norm_piece = lax.dynamic_slice_in_dim(norm_step, norm_start, norm_piece_size, 0)
    weight_updates = jnp.concatenate(
        [step_value.reshape(-1) for step_value in new_steps] + [norm_piece], axis=0
    ).reshape(1, 1, -1)
    layer_out = jnp.transpose(
        layer_share.astype(jnp.bfloat16).reshape(tok_share, seqs_here, model_width), (1, 0, 2)
    )
    input_grad_out = jnp.transpose(input_grad.reshape(tok_share, seqs_here, model_width), (1, 0, 2))
    return (
        layer_out,
        input_grad_out,
        weight_grads[0],
        weight_grads[1],
        weight_grads[2],
        weight_grads[3],
        norm_grad,
        new_pairs[0],
        new_pairs[1],
        new_pairs[2],
        new_pairs[3],
        norm_state,
        weight_updates,
    )


def solution(mesh):
    return jax.shard_map(
        shards,
        mesh=mesh,
        in_specs=(
            P("fsdp", "context", None),
            P("fsdp", "context", None),
            P("fsdp", "context"),
            P(),
            P("fsdp", None, "tensor"),
            P("tensor", "fsdp"),
            P("fsdp", None, "tensor"),
            P("tensor", "fsdp"),
            P(),
            P(),
            P("context", "fsdp", None, "tensor"),
            P("context", "fsdp", None, "tensor"),
            P("context", "tensor", "fsdp"),
            P("context", "tensor", "fsdp"),
            P("context", "fsdp", None, "tensor"),
            P("context", "fsdp", None, "tensor"),
            P("context", "tensor", "fsdp"),
            P("context", "tensor", "fsdp"),
            P(),
            P(),
        ),
        out_specs=(
            P("fsdp", ("context", "tensor"), None),
            P("fsdp", ("context", "tensor"), None),
            P("fsdp", None, "tensor"),
            P("tensor", "fsdp"),
            P("fsdp", None, "tensor"),
            P("tensor", "fsdp"),
            P(),
            P(None, "fsdp", None, "tensor"),
            P(None, "tensor", "fsdp"),
            P(None, "fsdp", None, "tensor"),
            P(None, "tensor", "fsdp"),
            P(),
            P("fsdp", "tensor", None),
        ),
        check_vma=False,
    )
```

profile of v0, /device:TPU:26, one launch (start us, length us, event | category | flops | bytes accessed | tf_op | source)
XLA Modules:
  0.0 747.4 jit_solution(17472209932976165733)
XLA Ops:
  12.8 23.8 %all_gather.27 = bf16[768,3,192]{2,0,1:T(8,128)(2,1)S(1)} all-gather(bf16[192,3,192]{2,0,1:T(8,128)(2,1)S(1)} %convert_element_type.179), channel_id=1, replica_groups=mesh['fsdp'=4,'context'=2,'tensor'=4] {'fsdp'}, dimensions={0}, use_global_device_ids=true | all-gather | bytes 1105920 | tf_op jit(solution)/shard_map/all_gather | solution.py:256
  64.4 15.4 %all_gather.30 = bf16[192,768]{0,1:T(8,128)(2,1)} all-gather(bf16[192,192]{0,1:T(8,128)(2,1)S(1)} %copy.169), channel_id=1, replica_groups=mesh['fsdp'=4,'context'=2,'tensor'=4] {'fsdp'}, dimensions={1}, use_global_device_ids=true | all-gather | bytes 368640 | tf_op jit(solution)/shard_map/all_gather | solution.py:257
  86.6 32.2 %while.59 = (s32[]{:T(128)}, f32[2,512,3,64]{1,3,2,0:T(8,128)}, f32[2,3,512]{2,1,0:T(4,128)S(1)}, bf16[2,1024,384]{1,2,0:T(8,128)(2,1)}, s32[2,1024]{1,0:T(2,128...) while((s32[]{:T(128)}, f32[2,512,3,64]{1,3,2,0:T(8,128)}, ...), condition=%wide.region_11.12_spmd, body=%wide.region_0.11_spmd.sunk | while | flops 210542592 | bytes 15957138 | solution.py:290
  89.5 12.4 %while.62 = (s32[]{:T(128)}, f32[3,512]{1,0:T(4,128)S(1)}, f32[3,512]{1,0:T(4,128)S(1)}, f32[512,3,64]{0,2,1:T(8,128)S(1)}, s32[1024]{0:T(1024)S(1)}, /*index=5*...) while((s32[]{:T(128)}, f32[3,512]{1,0:T(4,128)S(1)}, ...), condition=%wide.region_10.10_spmd, body=%wide.region_3.9_spmd.sunk | while | flops 210441728 | bytes 12755301 | solution.py:122
  105.6 12.4 %while.62 = (s32[]{:T(128)}, f32[3,512]{1,0:T(4,128)S(1)}, f32[3,512]{1,0:T(4,128)S(1)}, f32[512,3,64]{0,2,1:T(8,128)S(1)}, s32[1024]{0:T(1024)S(1)}, /*index=5*...) while((s32[]{:T(128)}, f32[3,512]{1,0:T(4,128)S(1)}, ...), condition=%wide.region_10.10_spmd, body=%wide.region_3.9_spmd.sunk | while | flops 210441728 | bytes 12755301 | solution.py:122
  129.0 25.8 %reduce-scatter.14.cloned.1.call-done = bf16[256,768]{1,0:T(8,128)(2,1)} async-done(((bf16[1024,768]{1,0:T(8,128)(2,1)}), bf16[256,768]{1,0:T(8,128)(2,1)}) %reduce-scatter.14.cloned.1.call-update) | async-done | bytes 393232 | tf_op jit(solution)/shard_map/reduce_scatter | solution.py:294
  159.2 17.7 %all-gather.11.cloned.1.call-done = bf16[768,2,768]{2,0,1:T(8,128)(2,1)} async-done(((bf16[192,2,768]{2,0,1:T(8,128)(2,1)}), bf16[768,2,768]{2,0,1:T(8,128)(2,1)}) %all-gather.11.cloned.1.call-update) | async-done | bytes 2359312 | tf_op jit(solution)/shard_map/all_gather | solution.py:258
  181.1 18.2 %all-gather.9.cloned.1.call-done = bf16[1024,768]{1,0:T(8,128)(2,1)} async-done(((bf16[256,768]{1,0:T(8,128)(2,1)}), bf16[1024,768]{1,0:T(8,128)(2,1)}) %all-gather.9.cloned.1.call-update) | async-done | bytes 1572880 | tf_op jit(solution)/shard_map/all_gather | solution.py:308
  208.9 21.0 %all-gather.13.cloned.1.call-done = bf16[768,768]{0,1:T(8,128)(2,1)} async-done(((bf16[768,192]{0,1:T(8,128)(2,1)}), bf16[768,768]{0,1:T(8,128)(2,1)}) %all-gather.13.cloned.1.call-update) | async-done | bytes 1179664 | tf_op jit(solution)/shard_map/all_gather | solution.py:259
  243.5 19.8 %reduce-scatter.16.cloned.1.call-done = bf16[256,768]{1,0:T(8,128)(2,1)} async-done(((bf16[1024,768]{1,0:T(8,128)(2,1)}), bf16[256,768]{1,0:T(8,128)(2,1)}) %reduce-scatter.16.cloned.1.call-update) | async-done | bytes 393232 | tf_op jit(solution)/shard_map/reduce_scatter | solution.py:318
  267.5 19.6 %all-gather.15.cloned.1.call-done = bf16[1024,768]{1,0:T(8,128)(2,1)} async-done(((bf16[256,768]{1,0:T(8,128)(2,1)}), bf16[1024,768]{1,0:T(8,128)(2,1)}) %all-gather.15.cloned.1.call-update) | async-done | bytes 1572880 | tf_op jit(solution)/shard_map/all_gather | solution.py:336
  298.5 28.1 %reduce-scatter.18.cloned.1.call-done = bf16[256,768]{1,0:T(8,128)(2,1)} async-done(((bf16[1024,768]{1,0:T(8,128)(2,1)}), bf16[256,768]{1,0:T(8,128)(2,1)}) %reduce-scatter.18.cloned.1.call-update) | async-done | bytes 393232 | tf_op jit(solution)/shard_map/reduce_scatter | solution.py:347
  330.4 19.4 %all-gather.17.cloned.1.call-done = bf16[1024,768]{1,0:T(8,128)(2,1)} async-done(((bf16[256,768]{1,0:T(8,128)(2,1)}), bf16[1024,768]{1,0:T(8,128)(2,1)}) %all-gather.17.cloned.1.call-update) | async-done | bytes 1572880 | tf_op jit(solution)/shard_map/all_gather | solution.py:361
  357.1 59.7 %while.61 = (s32[]{:T(128)}, f32[2,512,3,64]{1,3,2,0:T(8,128)}, bf16[2,1024,384]{1,2,0:T(8,128)(2,1)}, bf16[2,1024,384]{1,2,0:T(8,128)(2,1)}, s32[2,1024]{1,0:T(...) while((s32[]{:T(128)}, f32[2,512,3,64]{1,3,2,0:T(8,128)}, ...), condition=%wide.region_33.34_spmd, body=%wide.region_24.33_spmd.sunk | while | flops 512624640 | bytes 31325480 | solution.py:387
  363.8 20.1 %while.63 = (s32[]{:T(128)}, f32[512,3,64]{0,2,1:T(8,128)S(1)}, bf16[1024,384]{0,1:T(8,128)(2,1)}, s32[1024]{0:T(1024)S(1)}, s32[]{:T(128)}, /*index=5*/s32[]{:T...) while((s32[]{:T(128)}, f32[512,3,64]{0,2,1:T(8,128)S(1)}, ...), condition=%wide.region_32.32_spmd, body=%wide.region_27.31_spmd.sunk | while | flops 512623616 | bytes 19098020 | solution.py:186
  393.6 20.1 %while.63 = (s32[]{:T(128)}, f32[512,3,64]{0,2,1:T(8,128)S(1)}, bf16[1024,384]{0,1:T(8,128)(2,1)}, s32[1024]{0:T(1024)S(1)}, s32[]{:T(128)}, /*index=5*/s32[]{:T...) while((s32[]{:T(128)}, f32[512,3,64]{0,2,1:T(8,128)S(1)}, ...), condition=%wide.region_32.32_spmd, body=%wide.region_27.31_spmd.sunk | while | flops 512623616 | bytes 19098020 | solution.py:186
  429.2 13.0 %reduce-scatter.20.cloned.1.call-done = bf16[2,512,384]{1,2,0:T(8,128)(2,1)} async-done(((bf16[2,1024,384]{1,2,0:T(8,128)(2,1)}), bf16[2,512,384]{1,2,0:T(8,128)(2,1)}) %reduce-scatter.20.cloned.1.call-update) | async-done | bytes 786448 | tf_op jit(solution)/shard_map/reduce_scatter | solution.py:390
  466.4 25.3 %reduce-scatter.28.cloned.1.call-done = bf16[192,576]{1,0:T(8,128)(2,1)} async-done(((bf16[768,576]{1,0:T(8,128)(2,1)}), bf16[192,576]{1,0:T(8,128)(2,1)}) %reduce-scatter.28.cloned.1.call-update) | async-done | bytes 221200
  493.5 29.0 %reduce-scatter.26.cloned.1.call-done = bf16[768,192]{0,1:T(8,128)(2,1)} async-done(((bf16[768,768]{0,1:T(8,128)(2,1)}), bf16[768,192]{0,1:T(8,128)(2,1)}) %reduce-scatter.26.cloned.1.call-update) | async-done | bytes 294928 | tf_op jit(solution)/shard_map/reduce_scatter | solution.py:428
  522.5 49.9 %reduce-scatter.24.cloned.1.call-done = bf16[192,2,768]{2,0,1:T(8,128)(2,1)} async-done(((bf16[768,2,768]{2,0,1:T(8,128)(2,1)}), bf16[192,2,768]{2,0,1:T(8,128)(2,1)}) %reduce-scatter.24.cloned.1.call-update) | async-done | bytes 589840 | tf_op jit(solution)/shard_map/reduce_scatter | solution.py:425
  579.6 41.1 %all-reduce.7.cloned.1.call-done = (bf16[192,3,192]{0,2,1:T(8,128)(2,1)}, bf16[192,2,768]{2,0,1:T(8,128)(2,1)}, bf16[192,192]{1,0:T(8,128)(2,1)}, bf16[768,192]{0,1:T(8,128)(2,1)}) async-done(((bf16[192,3,192]{0,2,1:T(8,128)(2,1)}, bf16[192,2,768]{2,0,1:T(8,128)(2,1)}, bf16[192,192]{1,0:T(8,128)(2,1)}, bf16[768,192]{0,1:T(8,128)(2,1)}), (bf16[192,3,192]{0,2,1:T(8,128)(2,1)}, bf16[192,2,768]{2,0,1:T(8,128)(2,1)}, ...) | async-done | bytes 1179664 | tf_op jit(solution)/shard_map/psum | solution.py:433
  630.5 40.8 %psum.67 = f32[4,768]{1,0:T(4,128)S(1)} all-reduce(f32[4,768]{1,0:T(4,128)S(1)} %pad_maximum_fusion.14), channel_id=1, replica_groups=mesh['fsdp'=4,'context'=2,'tensor'=4] {'fsdp','context','tensor'}, use_global_device_ids=true, to_apply=%region_48.49 | all-reduce | flops 3072 | bytes 24576 | tf_op jit(solution)/shard_map/psum | solution.py:439
  677.7 23.7 %all-reduce.5.cloned.1.call-done = (bf16[2,192,3,192]{1,3,2,0:T(8,128)(2,1)}, bf16[2,192,192]{2,1,0:T(8,128)(2,1)}, bf16[2,192,2,768]{3,1,2,0:T(8,128)(2,1)}, bf16[2,768,192]{1,2,0:T(8,128)(2,1)}) async-done(((bf16[2,192,3,192]{1,3,2,0:T(8,128)(2,1)}, bf16[2,192,192]{2,1,0:T(8,128)(2,1)}, bf16[2,192,2,768]{3,1,2,0:T(8,128)(2,1)}, bf16[2,768,192]{1,2,0:T(8,128)(2,1)}), (bf16[2,192,3,192]{1,3,2,0:T(8,128)(2,1)}, ...) | async-done | bytes 2359312 | tf_op jit(solution)/shard_map/psum | solution.py:22
  729.5 10.4 %reshape.351 = f32[1,1,590016]{2,1,0:T(1,128)} reshape(f32[590016]{0:T(1024)} %constant_dynamic-update-slice_fusion) | data formatting | bytes 4720128 | tf_op jit(solution)/shard_map/reshape | solution.py:462
  (463 shorter events, 303.4 us)
Async XLA Ops:
  8.0 72.8 %all-gather.7.cloned.1.call-start = ((), (), s32[]{:S(2)}) async-start(), calls=%async_computation.9 | async-start | bytes 2359296 | tf_op jit(solution)/shard_map/all_gather | solution.py:280
  11.1 115.6 %copy-start = (bf16[512,2,768]{2,1,0:T(2,128)(2,1)}, bf16[512,2,768]{2,1,0:T(2,128)(2,1)S(1)}, u32[]{:S(2)}) copy-start(bf16[512,2,768]{2,1,0:T(2,128)(2,1)S(1)} %copy.158) | copy-start | bytes 4718596
  53.3 101.5 %reduce-scatter.14.cloned.1.call-start = ((), (), s32[]{:S(2)}) async-start(), calls=%async_computation.10 | async-start | bytes 1966080 | tf_op jit(solution)/shard_map/reduce_scatter | solution.py:294
  125.7 51.2 %all-gather.11.cloned.1.call-start = ((), (), s32[]{:S(2)}) async-start(), calls=%async_computation.12 | async-start | bytes 2949120 | tf_op jit(solution)/shard_map/all_gather | solution.py:258
  126.7 72.7 %all-gather.9.cloned.1.call-start = ((), (), s32[]{:S(2)}) async-start(), calls=%async_computation.11 | async-start | bytes 1966080 | tf_op jit(solution)/shard_map/all_gather | solution.py:308
  156.1 107.2 %copy-start.64 = (f32[256]{0:T(256)}, f32[256]{0:T(256)S(1)}, u32[]{:S(2)}) copy-start(f32[256]{0:T(256)S(1)} %broadcast_multiply_fusion.5) | copy-start | bytes 3076
  157.3 105.9 %copy-start.66 = (f32[256]{0:T(256)}, f32[256]{0:T(256)S(1)}, u32[]{:S(2)}) copy-start(f32[256]{0:T(256)S(1)} %add_rsqrt_fusion.1) | copy-start | bytes 3076
  158.3 71.5 %all-gather.13.cloned.1.call-start = ((), (), s32[]{:S(2)}) async-start(), calls=%async_computation.13 | async-start | bytes 1474560 | tf_op jit(solution)/shard_map/all_gather | solution.py:259
  159.2 104.1 %reduce-scatter.16.cloned.1.call-start = ((), (), s32[]{:S(2)}) async-start(), calls=%async_computation.14 | async-start | bytes 1966080 | tf_op jit(solution)/shard_map/reduce_scatter | solution.py:318
  234.2 52.9 %all-gather.15.cloned.1.call-start = ((), (), s32[]{:S(2)}) async-start(), calls=%async_computation.15 | async-start | bytes 1966080 | tf_op jit(solution)/shard_map/all_gather | solution.py:336
  267.5 59.1 %reduce-scatter.18.cloned.1.call-start = ((), (), s32[]{:S(2)}) async-start(), calls=%async_computation.16 | async-start | bytes 1966080 | tf_op jit(solution)/shard_map/reduce_scatter | solution.py:347
  298.5 51.3 %all-gather.17.cloned.1.call-start = ((), (), s32[]{:S(2)}) async-start(), calls=%async_computation.17 | async-start | bytes 1966080 | tf_op jit(solution)/shard_map/all_gather | solution.py:361
  330.1 112.0 %reduce-scatter.20.cloned.1.call-start = ((), (), s32[]{:S(2)}) async-start(), calls=%async_computation.18 | async-start | bytes 2359296 | tf_op jit(solution)/shard_map/reduce_scatter | solution.py:390
  416.8 47.8 %reduce-scatter.30.cloned.1.call-start = ((), (), s32[]{:S(2)}) async-start(), calls=%async_computation.23 | async-start | bytes 491520
  429.1 62.6 %reduce-scatter.28.cloned.1.call-start = ((), (), s32[]{:S(2)}) async-start(), calls=%async_computation.22 | async-start | bytes 1228800
  453.9 68.7 %reduce-scatter.26.cloned.1.call-start = ((), (), s32[]{:S(2)}) async-start(), calls=%async_computation.21 | async-start | bytes 1474560 | tf_op jit(solution)/shard_map/reduce_scatter | solution.py:428
  457.8 114.6 %reduce-scatter.24.cloned.1.call-start = ((), (), s32[]{:S(2)}) async-start(), calls=%async_computation.20 | async-start | bytes 2949120 | tf_op jit(solution)/shard_map/reduce_scatter | solution.py:425
  464.5 108.0 %copy-start.10 = (bf16[768,3,192]{2,0,1:T(8,128)(2,1)S(1)}, bf16[768,3,192]{2,0,1:T(8,128)(2,1)}, u32[]{:S(2)}) copy-start(bf16[768,3,192]{2,0,1:T(8,128)(2,1)} %copy-done.9) | copy-start | bytes 2654212
  464.5 108.0 %copy-start.54 = (bf16[1024,3,64]{0,2,1:T(8,128)(2,1)S(1)}, bf16[1024,3,64]{0,2,1:T(8,128)(2,1)}, u32[]{:S(2)}) copy-start(bf16[1024,3,64]{0,2,1:T(8,128)(2,1)} %copy-done.53) | copy-start | bytes 1179652
  464.5 108.0 %copy-start.56 = (bf16[1024,3,64]{0,2,1:T(8,128)(2,1)S(1)}, bf16[1024,3,64]{0,2,1:T(8,128)(2,1)}, u32[]{:S(2)}) copy-start(bf16[1024,3,64]{0,2,1:T(8,128)(2,1)} %copy-done.55) | copy-start | bytes 1179652
  464.6 156.1 %all-reduce.7.cloned.1.call-start = ((), (), s32[]{:S(2)}) async-start(), calls=%async_computation.25 | async-start | bytes 2555904 | tf_op jit(solution)/shard_map/psum | solution.py:433
  572.5 102.7 %reduce-scatter.22.cloned.1.call-start = ((), (), s32[]{:S(2)}) async-start(), calls=%async_computation.19 | async-start | bytes 1966080 | tf_op jit(solution)/shard_map/reduce_scatter | solution.py:406
  575.2 46.4 %copy-start.60 = (f32[1,192,192]{2,1,0:T(8,128)S(1)}, f32[1,192,192]{2,1,0:T(8,128)}, u32[]{:S(2)}) copy-start(f32[1,192,192]{2,1,0:T(8,128)} %param.45) | copy-start | bytes 442372
  575.3 126.1 %all-reduce.5.cloned.1.call-start = ((), (), s32[]{:S(2)}) async-start(), calls=%async_computation.24 | async-start | bytes 5111808 | tf_op jit(solution)/shard_map/psum | solution.py:22
  (74 other events, 558.4 us)
Sparse Core Ops, SparseCore 0:
  53.5 27.2 all-gather.6
  125.8 28.9 reduce-scatter.13
  234.3 28.8 reduce-scatter.15
  298.6 27.9 reduce-scatter.17
  416.9 25.2 reduce-scatter.19
  444.9 18.7 reduce-scatter.29
  466.5 25.1 reduce-scatter.27
  494.6 27.8 reduce-scatter.25
  525.4 47.0 reduce-scatter.23
  575.4 45.2 all-reduce.6
  627.5 73.8 all-reduce.4
Sparse Core Ops, SparseCore 1:
  128.3 48.5 all-gather.10
  178.9 20.4 all-gather.8
  201.4 28.4 all-gather.12
  267.5 19.5 all-gather.14
  330.2 19.5 all-gather.16
  576.4 28.9 reduce-scatter.21
where the time goes:
time: 761 us; the launch traced here: 747 us
  waiting for transfers between devices  353 us (46%)
  local copies, waits for them, and re-layouts  133 us (17%)
  blocking collectives  84.3 us (11%)
  matrix products  73.3 us (10%)
  other arithmetic  61.9 us (8%)
  loops' own time  21.2 us (3%)
  between operations  19.4 us (3%)
    reduce_scatter x1, waiting for transfers between devices, shards(): lax.psum_scatter(grad_terms[2].astype(jnp.bfloat16), 'fsdp', scatter_dime...  49.9 us
    psum x1, waiting for transfers between devices, shards(): lax.psum(grouped[0].astype(jnp.bfloat16), 'context').astype(jnp.float32)  41.1 us
    psum x1, blocking collectives, shards(): norm_grad = lax.psum(norm_terms, ('fsdp', 'context', 'tensor'))  40.8 us
    unnamed x176, local copies, waits for them, and re-layouts  35.9 us
    reduce_scatter x1, waiting for transfers between devices, shards(): lax.psum_scatter(grad_terms[3].astype(jnp.bfloat16), 'fsdp', scatter_dime...  29 us
    reduce_scatter x1, waiting for transfers between devices, shards(): lax.psum_scatter(jnp.einsum('rgf,dgf->rd', rows_of(grad_gate_up, jnp.int3...  28.1 us
    reduce_scatter x1, waiting for transfers between devices, shards(): lax.psum_scatter(jnp.dot(rows_of(attended_low, jnp.int32(0), share_rows *...  25.8 us
    unnamed x19, waiting for transfers between devices  25.6 us
  transfers between devices with their start and end apart: 17, of which 15 were waited for; matrix products, arithmetic and copies ran while one was open for 12% of the time, Pallas kernels for 0%

commit v1 on v0

v1 whole, which is shorter than its diff:
```python
import functools

import jax
import jax.numpy as jnp
from jax import lax
from jax.experimental import pallas as pl
from jax.experimental.pallas import tpu as pltpu
from jax.sharding import PartitionSpec as P

HD = 64

NEGATIVE = -1e30
EPSILON = 1e-05
ROPE_BASE = 1000.0
BETA_ONE = 0.9
BETA_TWO = 0.999
ADAM_EPS = 1e-08
ADAM_STEP = 3.0
RATE = 0.03
DECAY = 0.1

F32 = jnp.float32
BF16 = jnp.bfloat16
MESH = pl.DeviceIdType.MESH
NN = (((1,), (0,)), ((), ()))
NT = (((1,), (1,)), ((), ()))
TN = (((0,), (0,)), ((), ()))


def mm(left, right, dims):
    return lax.dot_general(left, right, dims, preferred_element_type=F32)


def swap_halves(values):
    lane = lax.broadcasted_iota(jnp.int32, values.shape, 1)
    low_half = lane % HD < HD // 2
    return jnp.where(
        low_half,
        pltpu.roll(values, 128 - HD // 2, 1),
        pltpu.roll(values, HD // 2, 1),
    )


def mean_of(values):
    return jnp.sum(values, axis=-1, keepdims=True) * (1.0 / values.shape[-1])


def normalize(values, gain_row, bias_row):
    center = values - mean_of(values)
    inverse_std = lax.rsqrt(mean_of(center * center) + EPSILON)
    unit = center * inverse_std
    return unit * gain_row + bias_row, unit, inverse_std


def norm_back(gradient, unit, inverse_std, gain_row):
    scaled = gradient * gain_row
    return inverse_std * (scaled - mean_of(scaled) - unit * mean_of(scaled * unit))


class Pack:
    pass


def layer_kernel(dims, *refs):
    S, T, D, C, F, NF, NC, NT4 = dims
    TS = T // NT4
    DB = D // NF
    QW, KW = 256, 384
    H = C // HD
    KS = min(max(NC - 1, 1), 2)
    scale = HD ** (-0.5)
    (
        tok, cot, ids_in, wq_in, wo_in, wg_in, wd_in, gains, biases, cos_t, sin_t,
        layer_out, input_grad, gq_out, go_out, gg_out, gd_out, norm_out,
        wq, wo, wg, wd, ids_all, q_ref, kv, att, tot, am, al, acc, bias_ref, vt,
        rsend, rsb, rs2, rs2r, ag1, ag2, ag3, hid, gb,
        n1, unit1, inv1, datt, dlt, dqt, dk, dv, kvg_s, kvg_r, kv_own, qb,
        gsq, gso, gsg, gsd, grq, gro, grg, grd, xq, xo, xg, xd, nsum_t, nsum_c, nsum_f, cot_v,
        w_ss, w_rs, kv_ss, kv_rs, id_ss, id_rs, rs_ss, rs_rs, ag_ss, ag_rs,
        kvg_ss, kvg_rs, gr_ss, gr_rs, x_ss, x_rs, n_ss, n_rs, loc_sem,
    ) = refs

    z, x, t = lax.axis_index("fsdp"), lax.axis_index("context"), lax.axis_index("tensor")
    core, yy = t % 2, t // 2
    t_core = yy * 2 + (1 - core)
    t_y = (1 - yy) * 2 + core
    t_diag = (1 - yy) * 2 + (1 - core)

    def remote(src, dst, ssem, rsem, axis, index):
        return pltpu.make_async_remote_copy(
            src_ref=src, dst_ref=dst, send_sem=ssem, recv_sem=rsem,
            device_id={axis: index}, device_id_type=MESH,
        )

    barrier = pltpu.get_barrier_semaphore()
    for d in range(1, NF):
        pl.semaphore_signal(barrier, inc=1, device_id={"fsdp": (z + d) % NF}, device_id_type=MESH)
    for d in range(1, NC):
        pl.semaphore_signal(barrier, inc=1, device_id={"context": (x + d) % NC}, device_id_type=MESH)
    for d in range(1, NT4):
        pl.semaphore_signal(barrier, inc=1, device_id={"tensor": (t + d) % NT4}, device_id_type=MESH)

    cot_copy = pltpu.make_async_copy(
        cot.at[:, pl.ds(pl.multiple_of(t * TS, TS), TS), :], cot_v, loc_sem.at[0]
    )
    cot_copy.start()

    def own_rows(index):
        return pl.ds(pl.multiple_of(index * DB, DB), DB)

    def pad_cols(values, left, right):
        parts = []
        if left:
            parts.append(jnp.zeros((values.shape[0], left), values.dtype))
        parts.append(values)
        if right:
            parts.append(jnp.zeros((values.shape[0], right), values.dtype))
        return jnp.concatenate(parts, axis=1)

    wq[own_rows(z), :] = jnp.concatenate(
        [
            pad_cols(wq_in[:, 0, :], 0, QW - C),
            jnp.concatenate([wq_in[:, 1, :], wq_in[:, 2, :]], axis=1),
        ],
        axis=1,
    ).astype(BF16)

    pl.semaphore_wait(barrier, NF - 1 + NC - 1 + NT4 - 1)

    def gather(buffer, slot):
        copies = []
        for d in range(1, NF):
            copies.append(
                remote(
                    buffer.at[own_rows(z), :], buffer.at[own_rows(z), :],
                    w_ss.at[slot, d - 1], w_rs.at[slot, d - 1], "fsdp", (z + d) % NF,
                )
            )
        for c in copies:
            c.start()
        return copies

    def wait_recv(copies):
        for c in copies:
            c.wait_recv()

    def wait_send(copies):
        for c in copies:
            c.wait_send()

    wq_copies = gather(wq, 0)

    ids_all[x] = ids_in[...]
    id_copies = []
    for d in range(1, NC):
        c = remote(
            ids_all.at[x], ids_all.at[x], id_ss.at[d - 1], id_rs.at[d - 1],
            "context", (x + d) % NC,
        )
        c.start()
        id_copies.append(c)

    def eye(n):
        return (
            lax.broadcasted_iota(jnp.int32, (n, n), 0)
            == lax.broadcasted_iota(jnp.int32, (n, n), 1)
        ).astype(F32).astype(BF16)

    wo_t = jnp.transpose(wo_in[...])
    wo[own_rows(z), :] = pad_cols(wo_t, HD, 0).astype(BF16)
    wd[own_rows(z), :] = jnp.transpose(wd_in[...]).astype(BF16)
    wg[own_rows(z), 0:F] = wg_in[:, 0, :].astype(BF16)
    wg[own_rows(z), F : 2 * F] = wg_in[:, 1, :].astype(BF16)

    wait_recv(wq_copies)
    wo_copies = gather(wo, 1)

    def rotate_pair(values, rows, sign):
        cosine, sine_rows = cos_t[rows, :], sin_t[rows, :] * sign
        lane = lax.broadcasted_iota(jnp.int32, cosine.shape, 1)
        head = lane < HD
        first, second = values[:, 0:128], values[:, 128:256]
        first = first * cosine + swap_halves(first) * sine_rows
        second = second * jnp.where(head, cosine, 1.0) + swap_halves(second) * jnp.where(
            head, sine_rows, 0.0
        )
        return first, second

    TR = min(256, T)

    def project(s):
        def tile(i, carry):
            rows = pl.ds(pl.multiple_of(i * TR, TR), TR)
            p = mm(tok[s, rows, :], wq[...], NN)
            q0, q1 = rotate_pair(p[:, 0:QW], rows, 1.0)
            q_ref[s, rows, 0:128] = q0.astype(BF16)
            q_ref[s, rows, 128:256] = q1.astype(BF16)
            k0, k1 = rotate_pair(p[:, QW : QW + 256], rows, 1.0)
            kv[x, s, rows, 0:128] = k0.astype(BF16)
            kv[x, s, rows, 128:256] = k1.astype(BF16)
            kv[x, s, rows, 256:384] = p[:, QW + 256 : QW + 384].astype(BF16)
            return carry

        lax.fori_loop(0, T // TR, tile, 0)
        for d in range(1, NC):
            kv_copy(s, d).start()

    def kv_copy(s, d):
        return remote(
            kv.at[x, s], kv.at[x, s], kv_ss.at[s, d - 1], kv_rs.at[s, d - 1],
            "context", (x + d) % NC,
        )

    def head_mask(h, offset):
        lane = lax.broadcasted_iota(jnp.int32, (1, 256), 1)
        return jnp.logical_and(lane >= offset + h * HD, lane < offset + (h + 1) * HD)

    def keep(values, mask):
        return jnp.where(mask, values, jnp.zeros_like(values))

    def doc_bias(j, s):
        key_ids = jnp.broadcast_to(ids_all[j, pl.ds(s, 1), :].astype(F32), (128, T))
        key_col = jnp.transpose(key_ids)[:, 0:1]
        query_row = ids_all[x, pl.ds(s, 1), :].astype(F32)
        bias_ref[...] = jnp.where(key_col == query_row, 0.0, NEGATIVE)

    eye256 = eye(256)

    def attend(s):
        am[...] = jnp.full(am.shape, NEGATIVE, F32)
        al[...] = jnp.zeros(al.shape, F32)
        acc[...] = jnp.zeros(acc.shape, F32)

        def block(d, carry):
            j = (x + NC - d) % NC
            doc_bias(j, s)
            vt[...] = mm(eye256, kv[j, s, :, 128:384], NT).astype(BF16)

            def head(h, inner):
                keys = keep(kv[j, s, :, 0:256], head_mask(h, 0))
                scores = mm(keys, q_ref[s], NT) * scale + bias_ref[...]
                row = pl.ds(h, 1)
                before = am[row, :]
                newest = jnp.maximum(before, jnp.max(scores, axis=0, keepdims=True))
                shrink = jnp.exp(before - newest)
                weights = jnp.exp(scores - newest)
                al[row, :] = al[row, :] * shrink + jnp.sum(weights, axis=0, keepdims=True)
                am[row, :] = newest
                rows = pl.ds(pl.multiple_of(h * HD, HD), HD)
                vrows = pl.ds(pl.multiple_of(HD + h * HD, HD), HD)
                acc[vrows, :] = acc[vrows, :] * shrink + mm(
                    vt[vrows, :], weights.astype(BF16), NN
                )
                return inner

            lax.fori_loop(0, H, head, 0)
            return carry

        block(0, 0)
        if NC > 1:
            for d in range(1, NC):
                kv_copy(s, d).wait_recv()
            if s == 0:
                wait_recv(id_copies)
            lax.fori_loop(1, NC, block, 0)
        for h in range(H):
            rows = slice(HD + h * HD, HD + (h + 1) * HD)
            acc[rows, :] = acc[rows, :] / al[h : h + 1, :]
        tot[s] = am[...] + jnp.log(jnp.maximum(al[...], 1e-37))
        att[s] = jnp.transpose(acc[...]).astype(BF16)

    def rs_copy(rnd, s, part):
        if part < 2:
            chip = 1 - yy if part == 0 else yy
            return remote(
                rsend.at[s, chip, 1 - core], rsb.at[s, chip],
                rs_ss.at[rnd, s, part], rs_rs.at[rnd, s, part], "tensor", t_core,
            )
        return remote(
            rs2.at[s], rs2r.at[s], rs_ss.at[rnd, s, 2], rs_rs.at[rnd, s, 2], "tensor", t_y
        )

    def rs_produce(rnd, s, product):
        if rnd > 0:
            for part in range(3):
                rs_copy(rnd - 1, s, part).wait_send()

        def tile(i, carry):
            chip = jnp.where(i < 2, 1 - yy, yy)
            other = jnp.where(i % 2 == 0, 1 - core, core)
            start = pl.multiple_of((chip * 2 + other) * TS, TS)
            rsend[s, chip, other] = product(s, pl.ds(start, TS)).astype(BF16)
            return carry

        lax.fori_loop(0, 2, tile, 0)
        rs_copy(rnd, s, 0).start()
        lax.fori_loop(2, 4, tile, 0)
        rs_copy(rnd, s, 1).start()

    def rs_middle(rnd, s):
        rs_copy(rnd, s, 0).wait_recv()
        rs2[s] = (
            rsend[s, 1 - yy, core].astype(F32) + rsb[s, 1 - yy].astype(F32)
        ).astype(BF16)
        rs_copy(rnd, s, 2).start()

    def rs_finish(rnd, s):
        rs_copy(rnd, s, 1).wait_recv()
        rs_copy(rnd, s, 2).wait_recv()
        return rsend[s, yy, core].astype(F32) + rsb[s, yy].astype(F32) + rs2r[s].astype(F32)

    def ag_copy(rnd, buffer, s, part):
        if part == 0:
            return remote(
                buffer.at[s, t], buffer.at[s, t],
                ag_ss.at[rnd, s, 0], ag_rs.at[rnd, s, 0], "tensor", t_core,
            )
        if part == 1:
            return remote(
                buffer.at[s, t], buffer.at[s, t],
                ag_ss.at[rnd, s, 1], ag_rs.at[rnd, s, 1], "tensor", t_y,
            )
        return remote(
            buffer.at[s, t_y], buffer.at[s, t_y],
            ag_ss.at[rnd, s, 2], ag_rs.at[rnd, s, 2], "tensor", t_core,
        )

    def ag_start(rnd, buffer, s):
        ag_copy(rnd, buffer, s, 1).start()
        ag_copy(rnd, buffer, s, 0).start()

    def ag_middle(rnd, buffer, s):
        ag_copy(rnd, buffer, s, 1).wait_recv()
        ag_copy(rnd, buffer, s, 2).start()

    def ag_finish(rnd, buffer, s):
        ag_copy(rnd, buffer, s, 0).wait_recv()
        ag_copy(rnd, buffer, s, 2).wait_recv()

    def out_product(s, rows):
        return mm(att[s, rows, :], wo[...], NT)

    def first_norm(s):
        share = pl.ds(pl.multiple_of(t * TS, TS), TS)
        values = tok[s, share, :].astype(F32) + rs_finish(0, s)
        normed, unit, inverse = normalize(values, gains[0:1, :], biases[0:1, :])
        n1[s] = normed
        unit1[s] = unit
        inv1[s] = jnp.broadcast_to(inverse, (TS, 128))
        ag1[s, t] = normed.astype(BF16)
        ag_start(0, ag1, s)

    def sigmoid(v):
        return 1.0 / (1.0 + jnp.exp(-v))

    def gate_up(s):
        def tile(i, carry):
            rows = pl.ds(pl.multiple_of(i * TS, TS), TS)
            both = mm(ag1[s, i], wg[...], NN)
            gate, up = both[:, 0:F], both[:, F : 2 * F]
            gb[s, rows, 0:F] = gate.astype(BF16)
            gb[s, rows, F : 2 * F] = up.astype(BF16)
            hid[s, rows, :] = (gate * sigmoid(gate) * up).astype(BF16)
            return carry

        lax.fori_loop(0, NT4, tile, 0)

    def down_product(s, rows):
        return mm(hid[s, rows, :], wd[...], NT)

    def second_norm(s):
        values = n1[s] + rs_finish(1, s)
        out, unit, inverse = normalize(values, gains[1:2, :], biases[1:2, :])
        layer_out[s] = out.astype(BF16)
        grad = cot_v[s].astype(F32)
        sums = (jnp.sum(grad * unit, axis=0, keepdims=True), jnp.sum(grad, axis=0, keepdims=True))
        add_sums(s, 1, sums)
        back = norm_back(grad, unit, inverse, gains[1:2, :])
        n1[s] = back
        ag2[s, t] = back.astype(BF16)
        ag_start(1, ag2, s)

    def add_sums(s, row, sums):
        for k in range(2):
            at = slice(row + 2 * k, row + 2 * k + 1)
            if s == 0:
                nsum_t[t, at, :] = sums[k]
            else:
                nsum_t[t, at, :] = nsum_t[t, at, :] + sums[k]

    def hidden_back(s):
        def tile(i, carry):
            rows = pl.ds(pl.multiple_of(i * TS, TS), TS)
            grad = mm(ag2[s, i], wd[...], NN)
            gate = gb[s, rows, 0:F].astype(F32)
            up = gb[s, rows, F : 2 * F].astype(F32)
            sig = sigmoid(gate)
            act = gate * sig
            gb[s, rows, 0:F] = (grad * up * (sig + act * (1.0 - sig))).astype(BF16)
            gb[s, rows, F : 2 * F] = (grad * act).astype(BF16)
            return carry

        lax.fori_loop(0, NT4, tile, 0)

    def gate_product(s, rows):
        return mm(gb[s, rows, :], wg[...], NT)

    def first_norm_back(s):
        grad = n1[s] + rs_finish(2, s)
        unit = unit1[s]
        sums = (jnp.sum(grad * unit, axis=0, keepdims=True), jnp.sum(grad, axis=0, keepdims=True))
        add_sums(s, 0, sums)
        back = norm_back(grad, unit, inv1[s, :, 0:1], gains[0:1, :])
        n1[s] = back
        ag3[s, t] = back.astype(BF16)
        ag_start(2, ag3, s)

    def weight_grad(dest, left_of, right):
        def tile(i, carry):
            columns = pl.ds(pl.multiple_of(i * 128, 128), 128)
            dest[columns, :] = mm(left_of(columns), right, TN).astype(BF16)
            return carry

        lax.fori_loop(0, D // 128, tile, 0)

    def reduce_start(slot, source, landing):
        for d in range(1, NF):
            reduce_copy(slot, source, landing, d).start()

    def reduce_copy(slot, source, landing, d):
        to = (z + d) % NF
        return remote(
            source.at[own_rows(to), :], landing.at[d - 1],
            gr_ss.at[slot, d - 1], gr_rs.at[slot, d - 1], "fsdp", to,
        )

    def reduce_middle(slot, source, landing, crossing):
        for d in range(1, NF):
            reduce_copy(slot, source, landing, d).wait_recv()
        total = source[own_rows(z), :].astype(F32)
        for d in range(1, NF):
            total = total + landing[d - 1].astype(F32)
        crossing[x] = total.astype(BF16)
        for d in range(1, NC):
            cross_copy(slot, crossing, d).start()

    def cross_copy(slot, crossing, d):
        return remote(
            crossing.at[x], crossing.at[x],
            x_ss.at[slot, d - 1], x_rs.at[slot, d - 1], "context", (x + d) % NC,
        )

    def reduce_finish(slot, source, landing, crossing, out):
        for d in range(1, NC):
            cross_copy(slot, crossing, d).wait_recv()
        total = crossing[0].astype(F32)
        for i in range(1, NC):
            total = total + crossing[i].astype(F32)
        out[...] = total
        for d in range(1, NC):
            cross_copy(slot, crossing, d).wait_send()
        for d in range(1, NF):
            reduce_copy(slot, source, landing, d).wait_send()

    def norm_copy(buffer, axis, me, count, base, d):
        return remote(
            buffer.at[me], buffer.at[me], n_ss.at[base + d - 1], n_rs.at[base + d - 1],
            axis, (me + d) % count,
        )

    norm_levels = (
        (nsum_t, "tensor", t, NT4, 0),
        (nsum_c, "context", x, NC, NT4 - 1),
        (nsum_f, "fsdp", z, NF, NT4 - 1 + NC - 1),
    )

    def norm_start(level):
        for d in range(1, norm_levels[level][3]):
            norm_copy(*norm_levels[level], d).start()

    def norm_total(level):
        buffer, count = norm_levels[level][0], norm_levels[level][3]
        for d in range(1, count):
            norm_copy(*norm_levels[level], d).wait_recv()
        total = buffer[0]
        for i in range(1, count):
            total = total + buffer[i]
        return total

    def attended_back(s):
        def tile(i, carry):
            rows = pl.ds(pl.multiple_of(i * TS, TS), TS)
            datt[s, rows, :] = mm(ag3[s, i], wo[...], NN).astype(BF16)
            return carry

        lax.fori_loop(0, NT4, tile, 0)
        both = datt[s].astype(F32) * att[s].astype(F32)
        head_row = lax.broadcasted_iota(jnp.int32, (8, 256), 0)
        lane = lax.broadcasted_iota(jnp.int32, (8, 256), 1)
        chooser = (lane // HD == head_row + 1).astype(F32)
        dlt[s] = lax.dot_general(
            chooser, both, NT, precision=lax.Precision.HIGHEST, preferred_element_type=F32
        )

    def kvg_copy(s, d):
        return remote(
            kvg_s.at[(d - 1) % KS, s], kvg_r.at[d - 1, s],
            kvg_ss.at[d - 1, s], kvg_rs.at[d - 1, s], "context", (x + NC - d) % NC,
        )

    def attend_back(s):
        dqt[...] = jnp.zeros(dqt.shape, F32)

        def block(d):
            j = (x + NC - d) % NC
            doc_bias(j, s)
            vt[...] = mm(eye256, kv[j, s, :, 0:256], NT).astype(BF16)
            dk[...] = jnp.zeros(dk.shape, F32)
            dv[...] = jnp.zeros(dv.shape, F32)

            def head(h, inner):
                key_mask, value_mask = head_mask(h, 0), head_mask(h, HD)
                keys = keep(kv[j, s, :, 0:256], key_mask)
                row = pl.ds(h, 1)
                scores = mm(keys, q_ref[s], NT) * scale + bias_ref[...]
                probs = jnp.exp(scores - tot[s, row, :])
                dv[...] += mm(probs.astype(BF16), keep(datt[s], value_mask), NN)
                grad_probs = mm(keep(kv[j, s, :, 128:384], value_mask), datt[s], NT)
                grads = (probs * (grad_probs - dlt[s, row, :])).astype(BF16)
                dk[...] += mm(grads, keep(q_ref[s], key_mask), NN)
                rows = pl.ds(pl.multiple_of(h * HD, HD), HD)
                dqt[rows, :] += mm(vt[rows, :], grads, NN)
                return inner

            lax.fori_loop(0, H, head, 0)
            first = dk[:, 0:128] * scale
            second = dk[:, 128:256] * scale + dv[:, 0:128]
            return first, second, dv[:, 128:256]

        def far(d, carry):
            parts = block(d)
            if NC - 1 > KS:

                @pl.when(d > KS)
                def _():
                    kvg_copy(s, d - KS).wait_send()

            for k in range(3):
                kvg_s[(d - 1) % KS, s, :, k * 128 : (k + 1) * 128] = parts[k].astype(BF16)
            kvg_copy(s, d).start()
            return carry

        if NC > 1:
            lax.fori_loop(1, NC, far, 0)
        parts = block(0)
        for k in range(3):
            kv_own[s, :, k * 128 : (k + 1) * 128] = parts[k]
        grad = jnp.transpose(dqt[...]) * scale
        q0, q1 = rotate_pair(grad, slice(0, T), -1.0)
        qb[s, :, 0:128] = q0.astype(BF16)
        qb[s, :, 128:256] = q1.astype(BF16)

    def keys_back(s):
        for d in range(1, NC):
            kvg_copy(s, d).wait_recv()

        def column(k):
            cols = slice(k * 128, (k + 1) * 128)
            total = kv_own[s, :, cols]
            for d in range(1, NC):
                total = total + kvg_r[d - 1, s, :, cols].astype(F32)
            return total

        k0, k1 = rotate_pair(
            jnp.concatenate([column(0), column(1)], axis=1), slice(0, T), -1.0
        )
        qb[s, :, QW : QW + 128] = k0.astype(BF16)
        qb[s, :, QW + 128 : QW + 256] = k1.astype(BF16)
        qb[s, :, QW + 256 : QW + 384] = column(2).astype(BF16)

    def input_product(s, rows):
        return mm(qb[s, rows, :], wq[...], NT)

    def input_out(s):
        input_grad[s] = n1[s] + rs_finish(3, s)

    seqs = range(S)
    R = S * T

    for s in seqs:
        project(s)
    wait_recv(wo_copies)
    wg_copies = gather(wg, 2)
    wd_copies = gather(wd, 3)
    for s in seqs:
        attend(s)
        if s > 0:
            rs_middle(0, s - 1)
        rs_produce(0, s, out_product)
        if s > 0:
            first_norm(s - 1)
    rs_middle(0, S - 1)
    first_norm(S - 1)
    wait_recv(wg_copies)
    for s in seqs:
        ag_middle(0, ag1, s)
    for s in seqs:
        ag_finish(0, ag1, s)
        gate_up(s)
        if s == 0:
            wait_recv(wd_copies)
        rs_produce(1, s, down_product)
        if s > 0:
            rs_middle(1, s - 1)
    rs_middle(1, S - 1)
    cot_copy.wait()
    nsum_t[t] = jnp.zeros(nsum_t.shape[1:], F32)
    for s in seqs:
        second_norm(s)
    for s in seqs:
        ag_middle(1, ag2, s)
    for s in seqs:
        ag_finish(1, ag2, s)
        hidden_back(s)
        rs_produce(2, s, gate_product)
        if s > 0:
            rs_middle(2, s - 1)
    rs_middle(2, S - 1)
    flat_hid = hid[...].reshape(R, F)
    weight_grad(gsd, lambda c: ag2[:, :, :, c].reshape(R, 128), flat_hid)
    reduce_start(3, gsd, grd)
    for s in seqs:
        first_norm_back(s)
    norm_start(0)
    weight_grad(gsg, lambda c: ag1[:, :, :, c].reshape(R, 128), gb[...].reshape(R, 2 * F))
    reduce_start(2, gsg, grg)
    for s in seqs:
        ag_middle(2, ag3, s)
    for s in seqs:
        ag_finish(2, ag3, s)
        attended_back(s)
        if s == 0:
            nsum_c[x] = norm_total(0)
            norm_start(1)
        attend_back(s)
    nsum_f[z] = norm_total(1)
    norm_start(2)
    weight_grad(gso, lambda c: ag3[:, :, :, c].reshape(R, 128), att[...].reshape(R, 256))
    reduce_start(1, gso, gro)
    for s in seqs:
        keys_back(s)
        rs_produce(3, s, input_product)
        if s > 0:
            rs_middle(3, s - 1)
    rs_middle(3, S - 1)
    weight_grad(gsq, lambda c: tok[:, :, c].reshape(R, 128), qb[...].reshape(R, QW + KW))
    reduce_start(0, gsq, grq)
    norm_out[...] = norm_total(2)
    reduce_middle(3, gsd, grd, xd)
    reduce_middle(2, gsg, grg, xg)
    reduce_middle(1, gso, gro, xo)
    for s in seqs:
        input_out(s)
    reduce_middle(0, gsq, grq, xq)
    reduce_finish(3, gsd, grd, xd, gd_out)
    reduce_finish(2, gsg, grg, xg, gg_out)
    reduce_finish(1, gso, gro, xo, go_out)
    reduce_finish(0, gsq, grq, xq, gq_out)

    for copies in (wq_copies, wo_copies, wg_copies, wd_copies, id_copies):
        wait_send(copies)
    for s in seqs:
        for d in range(1, NC):
            kv_copy(s, d).wait_send()
            if d > NC - 1 - KS:
                kvg_copy(s, d).wait_send()
        for part in range(3):
            rs_copy(3, s, part).wait_send()
        for rnd, buffer in ((0, ag1), (1, ag2), (2, ag3)):
            for part in range(3):
                ag_copy(rnd, buffer, s, part).wait_send()
    for level in range(3):
        for d in range(1, norm_levels[level][3]):
            norm_copy(*norm_levels[level], d).wait_send()


def run_layer(tokens, cotangent, segment_ids, weights, norm_gains, norm_biases, cosine, sine_rows):
    qkv_weight, out_weight, gate_up_weight, down_weight = weights
    S, T, D = tokens.shape
    C, F = qkv_weight.shape[2], gate_up_weight.shape[2]
    NF, NC, NT4 = lax.axis_size("fsdp"), lax.axis_size("context"), lax.axis_size("tensor")
    TS, DB, KW, W = T // NT4, D // NF, 384, 640
    assert NT4 == 4 and C == 192
    vmem = pl.BlockSpec(memory_space=pltpu.VMEM)
    far = pl.BlockSpec(memory_space=pl.ANY)
    VM = pltpu.VMEM
    DMA = pltpu.SemaphoreType.DMA
    NX = max(NC - 1, 1)
    scratch = [
        VM((D, W), BF16), VM((D, 256), BF16), VM((D, 2 * F), BF16), VM((D, F), BF16),
        VM((NC, S, T), jnp.int32), VM((S, T, 256), BF16), VM((NC, S, T, KW), BF16),
        VM((S, T, 256), BF16), VM((S, 8, T), F32), VM((8, T), F32), VM((8, T), F32),
        VM((256, T), F32), VM((T, T), F32), VM((256, T), BF16),
        VM((S, 2, 2, TS, D), BF16), VM((S, 2, TS, D), BF16), VM((S, TS, D), BF16), VM((S, TS, D), BF16),
        VM((S, 4, TS, D), BF16), VM((S, 4, TS, D), BF16), VM((S, 4, TS, D), BF16),
        VM((S, T, F), BF16), VM((S, T, 2 * F), BF16),
        VM((S, TS, D), F32), VM((S, TS, D), F32), VM((S, TS, 128), F32),
        VM((S, T, 256), BF16), VM((S, 8, T), F32), VM((256, T), F32),
        VM((T, 256), F32), VM((T, 256), F32), VM((min(NX, 2), S, T, KW), BF16), VM((NX, S, T, KW), BF16),
        VM((S, T, KW), F32), VM((S, T, W), BF16),
        VM((D, W), BF16), VM((D, 256), BF16), VM((D, 2 * F), BF16), VM((D, F), BF16),
        VM((NF - 1, DB, W), BF16), VM((NF - 1, DB, 256), BF16), VM((NF - 1, DB, 2 * F), BF16),
        VM((NF - 1, DB, F), BF16),
        VM((NC, DB, W), BF16), VM((NC, DB, 256), BF16), VM((NC, DB, 2 * F), BF16), VM((NC, DB, F), BF16),
        VM((NT4, 8, D), F32), VM((NC, 8, D), F32), VM((NF, 8, D), F32), VM((S, TS, D), BF16),
        DMA((4, NF - 1)), DMA((4, NF - 1)), DMA((S, NX)), DMA((S, NX)), DMA((NX,)), DMA((NX,)),
        DMA((4, S, 3)), DMA((4, S, 3)), DMA((3, S, 3)), DMA((3, S, 3)),
        DMA((NX, S)), DMA((NX, S)), DMA((4, NF - 1)), DMA((4, NF - 1)), DMA((4, NX)), DMA((4, NX)),
        DMA((NT4 + NC + NF,)), DMA((NT4 + NC + NF,)), DMA((1,)),
    ]
    outs = (
        jax.ShapeDtypeStruct((S, TS, D), BF16),
        jax.ShapeDtypeStruct((S, TS, D), F32),
        jax.ShapeDtypeStruct((DB, W), F32),
        jax.ShapeDtypeStruct((DB, 256), F32),
        jax.ShapeDtypeStruct((DB, 2 * F), F32),
        jax.ShapeDtypeStruct((DB, F), F32),
        jax.ShapeDtypeStruct((8, D), F32),
    )
    return pl.pallas_call(
        functools.partial(layer_kernel, (S, T, D, C, F, NF, NC, NT4)),
        out_shape=outs,
        in_specs=[vmem, far] + [vmem] * 9,
        out_specs=[vmem] * len(outs),
        scratch_shapes=scratch,
        compiler_params=pltpu.CompilerParams(
            collective_id=0, has_side_effects=True, vmem_limit_bytes=67043328
        ),
        name="layer",
    )(
        tokens, cotangent, segment_ids, qkv_weight, out_weight, gate_up_weight, down_weight,
        norm_gains, norm_biases, cosine, sine_rows,
    )


def from_root(block, axis, owner):
    block = jnp.where(lax.axis_index(axis) == owner, block, jnp.zeros_like(block))
    return lax.psum(block, axis)


def moment_pair(gradient, moment, square):
    moment_new = BETA_ONE * moment + (1.0 - BETA_ONE) * gradient
    square_new = BETA_TWO * square + (1.0 - BETA_TWO) * gradient * gradient
    return jnp.stack([moment_new, square_new])


def step_of(pair_new, master, decay_rate):
    corrected = pair_new[0] / (1.0 - BETA_ONE**ADAM_STEP)
    scaled = pair_new[1] / (1.0 - BETA_TWO**ADAM_STEP)
    return -RATE * (corrected / (jnp.sqrt(scaled) + ADAM_EPS) + decay_rate * master)


def shards(
    tokens, cotangent, segment_ids, owner, qkv_weight, out_weight, gate_up_weight, down_weight,
    norm_gains, norm_biases, qkv_moment, qkv_square, out_moment, out_square, gate_moment,
    gate_square, down_moment, down_square, norm_moment, norm_square,
):
    seqs_here, tok_here, model_width = tokens.shape
    head_cols = qkv_weight.shape[2]
    hidden_here = gate_up_weight.shape[2]
    tensor_size, fsdp_size = lax.axis_size("tensor"), lax.axis_size("fsdp")
    masters = (qkv_weight, out_weight, gate_up_weight, down_weight)
    moments = (
        (qkv_moment, qkv_square), (out_moment, out_square),
        (gate_moment, gate_square), (down_moment, down_square),
    )
    owned = [
        [
            from_root(slot[0].astype(BF16), "context", owner[k]).astype(F32)
            for slot in moments[k]
        ]
        for k in range(4)
    ]
    positions = (
        lax.axis_index("context") * tok_here + jnp.arange(tok_here, dtype=jnp.int32)
    ).astype(F32)
    frequency = jnp.power(F32(ROPE_BASE), -jnp.arange(0, HD, 2, dtype=F32) / HD)
    angles = positions[:, None] * frequency[None, :]
    cosine, sine_rows = jnp.cos(angles), jnp.sin(angles)
    cosine = jnp.concatenate([cosine] * 4, axis=1)
    sine_rows = jnp.concatenate([-sine_rows, sine_rows] * 2, axis=1)

    layer_out, input_grad, grad_q, grad_o, grad_g, grad_d, norm_sums = run_layer(
        tokens, cotangent, segment_ids, masters, norm_gains, norm_biases, cosine, sine_rows
    )
    rows = qkv_weight.shape[0]
    weight_grads = (
        jnp.concatenate([grad_q[:, :head_cols], grad_q[:, 256:]], axis=1).reshape(rows, 3, head_cols),
        jnp.transpose(grad_o[:, HD:]),
        grad_g.reshape(rows, 2, hidden_here),
        jnp.transpose(grad_d),
    )
    norm_grad = norm_sums[:4]
    new_pairs = [moment_pair(weight_grads[k], owned[k][0], owned[k][1]) for k in range(4)]
    new_steps = [step_of(new_pairs[k], masters[k], DECAY) for k in range(4)]
    norm_master = jnp.concatenate([norm_gains, norm_biases], axis=0)
    norm_state = moment_pair(norm_grad, norm_moment, norm_square)
    norm_step = step_of(norm_state, norm_master, 0.0).reshape(-1)
    piece = norm_step.shape[0] // (fsdp_size * tensor_size)
    start = (lax.axis_index("fsdp") * tensor_size + lax.axis_index("tensor")) * piece
    norm_piece = lax.dynamic_slice_in_dim(norm_step, start, piece, 0)
    weight_updates = jnp.concatenate(
        [value.reshape(-1) for value in new_steps] + [norm_piece], axis=0
    ).reshape(1, 1, -1)
    return (
        layer_out, input_grad, *weight_grads, norm_grad, *new_pairs, norm_state, weight_updates
    )


def solution(mesh):
    return jax.shard_map(
        shards,
        mesh=mesh,
        in_specs=(
            P("fsdp", "context", None),
            P("fsdp", "context", None),
            P("fsdp", "context"),
            P(),
            P("fsdp", None, "tensor"),
            P("tensor", "fsdp"),
            P("fsdp", None, "tensor"),
            P("tensor", "fsdp"),
            P(),
            P(),
            P("context", "fsdp", None, "tensor"),
            P("context", "fsdp", None, "tensor"),
            P("context", "tensor", "fsdp"),
            P("context", "tensor", "fsdp"),
            P("context", "fsdp", None, "tensor"),
            P("context", "fsdp", None, "tensor"),
            P("context", "tensor", "fsdp"),
            P("context", "tensor", "fsdp"),
            P(),
            P(),
        ),
        out_specs=(
            P("fsdp", ("context", "tensor"), None),
            P("fsdp", ("context", "tensor"), None),
            P("fsdp", None, "tensor"),
            P("tensor", "fsdp"),
            P("fsdp", None, "tensor"),
            P("tensor", "fsdp"),
            P(),
            P(None, "fsdp", None, "tensor"),
            P(None, "tensor", "fsdp"),
            P(None, "fsdp", None, "tensor"),
            P(None, "tensor", "fsdp"),
            P(),
            P("fsdp", "tensor", None),
        ),
        check_vma=False,
    )
```

time: 761 us -> 371 us (0.49)
  waiting for transfers between devices: 353 us -> 0.02 us
  Pallas kernels: 0 us -> 277 us
  local copies, waits for them, and re-layouts: 133 us -> 44.7 us
  blocking collectives: 84.3 us -> 0 us
  matrix products: 73.3 us -> 0 us
  other arithmetic: 61.9 us -> 24.2 us
  loops' own time: 21.2 us -> 0 us
    pallas_call x0 -> x1, Pallas kernels: none -> 277 us  [run_layer(): pl.pallas_call(functools.partial(layer_kernel, (S, T, D, C, F, NF, NC, NT...]
    reduce_scatter x7 -> x0, waiting for transfers between devices: 166 us -> none  [the longest x1 49.9 us: shards(): lax.psum_scatter(grad_terms[2].astype(jnp.bfloat16), 'fsdp', scatter_dime...]
    all_gather x6 -> x0, waiting for transfers between devices: 96.8 us -> none  [the longest x1 21 us: shards(): lax.all_gather(low_weights[3], 'fsdp', axis=1, tiled=True)]
    dot_general x40 -> x0, matrix products: 73.3 us -> none  [the longest x4 8.51 us: grad_visit(): jnp.einsum('qhd,khd->hqk', grad_part, value_rows, preferred_element_type=...]
    all_gather x3 -> x0, blocking collectives: 43.6 us -> none  [the longest x1 23.8 us: shards(): lax.all_gather(low_weights[0], 'fsdp', axis=0, tiled=True)]
    psum x1 -> x0, waiting for transfers between devices: 41.1 us -> none  [shards(): lax.psum(grouped[0].astype(jnp.bfloat16), 'context').astype(jnp.float32)]
    psum x1 -> x0, blocking collectives: 40.8 us -> none  [shards(): norm_grad = lax.psum(norm_terms, ('fsdp', 'context', 'tensor'))]
    unnamed x19 -> x1, waiting for transfers between devices: 25.6 us -> 0.02 us
  transfers between devices with their start and end apart: 17 -> 1, of which waited for: 15 -> 0; matrix products, arithmetic and copies ran while one was open for 12% -> 4% of each run, Pallas kernels for 0% -> 76%
where the time goes in v1:
time: 371 us; the launch traced here: 364 us
  Pallas kernels  277 us (75%)
  local copies, waits for them, and re-layouts  44.7 us (12%)
  other arithmetic  24.2 us (7%)
  between operations  17.6 us (5%)
    pallas_call x1, Pallas kernels, run_layer(): pl.pallas_call(functools.partial(layer_kernel, (S, T, D, C, F, NF, NC, NT...  277 us
    unnamed x87, local copies, waits for them, and re-layouts  19.4 us
    mul x5, other arithmetic, step_of(): -RATE * (corrected / (jnp.sqrt(scaled) + ADAM_EPS) + decay_rate * master)  13 us
    reshape x1, local copies, waits for them, and re-layouts, shards(): weight_updates = jnp.concatenate([value.reshape(-1) for value in new_step...  12 us
  transfers between devices with their start and end apart: 1, of which 0 were waited for; matrix products, arithmetic and copies ran while one was open for 4% of the time, Pallas kernels for 76%

profile of v1, /device:TPU:26, one launch (start us, length us, event | category | flops | bytes accessed | tf_op | source)
XLA Modules:
  0.0 363.9 jit_solution(10150151459931698441)
XLA Ops:
  7.2 1.4 fusion.20
  8.6 1.2 copy.64
  12.8 1.0 copy.66
  13.8 1.0 copy.67
  15.7 2.0 fusion.3
  19.3 1.0 copy-done.13
  20.3 1.3 copy.61.refs_3_
  21.6 1.1 copy.62.refs_6_
  22.8 1.0 fusion.12
  23.8 1.3 pad_maximum_fusion.5
  25.1 277.3 %layer.1 = (bf16[2,128,768]{2,1,0:T(8,128)(2,1)}, f32[2,128,768]{2,1,0:T(8,128)}, f32[192,640]{1,0:T(8,128)}, f32[192,256]{1,0:T(8,128)}, f32[192,1536]{1,0:T(8,...) custom-call(bf16[2,512,768]{2,1,0:T(8,128)(2,1)} %refs_0_.1, bf16[2,512,768]{2,1,0:T(8,128)(2,1)} %refs_1_.1, ...), custom_call_target="tpu_custom_call" | custom-call | tf_op jit(solution)/shard_map/layer/pallas_call | solution.py:730
  302.4 1.1 slice.29
  306.9 1.2 fusion.16
  308.7 1.1 copy.73
  311.4 2.5 add_multiply_fusion.2
  317.4 5.8 %add_multiply_fusion = (f32[192,2,768]{2,1,0:T(2,128)S(1)}, f32[1,192,2,768]{3,2,1,0:T(2,128)}, f32[1,192,2,768]{3,2,1,0:T(2,128)}) fusion(f32[192,2,768]{2,1,0:T(2,128)S(1)} %copy-done, f32[192,2,768]{2,1,0:T(2,128)S(1)} %reshape.95, bf16[192,2,768]{2,1,0:T(2,128)(2,1)} %get-tuple-element.71, bf16[192,2,768]{2,1,0:T(2,128)(2,1)} %get-tuple-element.70), kind=kLoop, calls=%fused_computation.5 | loop fusion | flops 4718592 | bytes 7077888 | tf_op jit(solution)/shard_map/mul | solution.py:760
  324.5 2.5 add_multiply_fusion.1
  327.0 2.4 copy.72
  329.4 2.3 reshape.99
  332.7 1.0 copy-done.15
  334.5 12.0 %reshape.101 = f32[1,1,590016]{2,1,0:T(1,128)} reshape(f32[590016]{0:T(1024)S(1)} %constant_dynamic-update-slice_fusion) | data formatting | bytes 4720128 | tf_op jit(solution)/shard_map/reshape | solution.py:814
  348.1 1.5 copy.75
  349.6 1.1 pad_maximum_fusion.2
  351.6 2.5 pad_maximum_fusion
  (103 shorter events, 19.6 us)
Async XLA Ops:
  7.2 2.7 copy-start.25
  7.2 304.2 %all-reduce.3.cloned.1.call-start = ((), (), s32[]{:S(2)}) async-start(), calls=%async_computation | async-start | bytes 5111808 | tf_op jit(solution)/shard_map/psum | solution.py:748
  9.9 5.8 %copy-start.17 = (f32[1,192,2,768]{3,2,1,0:T(2,128)S(1)}, f32[1,192,2,768]{3,2,1,0:T(2,128)}, u32[]{:S(2)}) copy-start(f32[1,192,2,768]{3,2,1,0:T(2,128)} %param.34) | copy-start | bytes 3538948
  9.9 5.8 %copy-start.18 = (f32[1,192,2,768]{3,2,1,0:T(2,128)S(1)}, f32[1,192,2,768]{3,2,1,0:T(2,128)}, u32[]{:S(2)}) copy-start(f32[1,192,2,768]{3,2,1,0:T(2,128)} %param.35) | copy-start | bytes 3538948
  15.7 2.0 copy-start.26
  15.7 2.0 copy-start.27
  19.3 2.3 copy-start.7
  302.4 2.0 copy-start.14
  302.4 2.3 copy-start.19
  306.8 10.6 %copy-start.1 = (f32[192,2,768]{2,1,0:T(2,128)}, f32[192,2,768]{2,1,0:T(2,128)S(1)}, u32[]{:S(2)}) copy-start(f32[192,2,768]{2,1,0:T(2,128)S(1)} %reshape.95) | copy-start | bytes 3538948
  306.9 2.9 copy-start.20
  306.9 3.9 %copy-start.32 = (f32[4,768]{1,0:T(4,128)S(1)}, f32[4,768]{1,0:T(4,128)}, u32[]{:S(2)}) copy-start(f32[4,768]{1,0:T(4,128)} %param.39) | copy-start | bytes 36868
  308.1 3.2 copy-start.33
  315.5 1.9 copy-start
  327.0 4.7 %copy-start.4 = (f32[590016]{0:T(1024)S(1)}, f32[590016]{0:T(1024)}, u32[]{:S(2)}) copy-start(f32[590016]{0:T(1024)} %constant_dynamic-update-slice_fusion.4) | copy-start | bytes 7080196
  334.5 12.0 %copy-start.23 = (f32[1,192,192]{1,2,0:T(8,128)S(1)}, f32[1,192,192]{1,2,0:T(8,128)}, u32[]{:S(2)}) copy-start(f32[1,192,192]{1,2,0:T(8,128)} %get-tuple-element.86) | copy-start | bytes 442372
  334.5 12.0 %copy-start.24 = (f32[1,192,192]{1,2,0:T(8,128)S(1)}, f32[1,192,192]{1,2,0:T(8,128)}, u32[]{:S(2)}) copy-start(f32[1,192,192]{1,2,0:T(8,128)} %get-tuple-element.87) | copy-start | bytes 442372
  348.1 1.5 copy-start.11
  348.1 1.5 copy-start.12
  349.5 1.7 copy-start.2
  349.6 2.1 copy-start.3
  351.6 2.5 copy-start.28
  351.6 3.3 copy-start.22
  354.1 1.6 copy-start.6
  (11 other events, 12.9 us)
Sparse Core Ops, SparseCore 0:
  19.4 81.0 all-reduce.2

commit v2 on v1

--- a/solution.py
+++ b/solution.py
@@ -1,4 +1,5 @@
 import functools
+import math
 
 import jax
 import jax.numpy as jnp
@@ -63,22 +64,39 @@
 
 def layer_kernel(dims, *refs):
     S, T, D, C, F, NF, NC, NT4 = dims
+    adam = NC == 2
+    refs = list(refs)
     TS = T // NT4
     DB = D // NF
     QW, KW = 256, 384
     H = C // HD
     KS = min(max(NC - 1, 1), 2)
     scale = HD ** (-0.5)
-    (
-        tok, cot, ids_in, wq_in, wo_in, wg_in, wd_in, gains, biases, cos_t, sin_t,
-        layer_out, input_grad, gq_out, go_out, gg_out, gd_out, norm_out,
-        wq, wo, wg, wd, ids_all, q_ref, kv, att, tot, am, al, acc, bias_ref, vt,
-        rsend, rsb, rs2, rs2r, ag1, ag2, ag3, hid, gb,
-        n1, unit1, inv1, datt, dlt, dqt, dk, dv, kvg_s, kvg_r, kv_own, qb,
-        gsq, gso, gsg, gsd, grq, gro, grg, grd, xq, xo, xg, xd, nsum_t, nsum_c, nsum_f, cot_v,
-        w_ss, w_rs, kv_ss, kv_rs, id_ss, id_rs, rs_ss, rs_rs, ag_ss, ag_rs,
-        kvg_ss, kvg_rs, gr_ss, gr_rs, x_ss, x_rs, n_ss, n_rs, loc_sem,
-    ) = refs
+    def take(count):
+        taken, refs[:] = refs[:count], refs[count:]
+        return taken
+
+    tok, cot, ids_in, wq_in, wo_in, wg_in, wd_in, gains, biases, cos_t, sin_t = take(11)
+    if adam:
+        moments = take(8)
+    layer_out, input_grad = take(2)
+    own_out, crosses = take(4), take(4)
+    norm_out = take(1)[0]
+    if adam:
+        lands = take(4)
+    wq, wo, wg, wd, ids_all, q_ref, kv, att, tot, am, al, acc, bias_ref, vt = take(14)
+    rsend, rsb, rs2, rs2r, ag1, ag2, ag3, hid, gb = take(9)
+    n1, unit1, inv1, datt, dlt, dk, dv, kvg_s, kvg_r, kv_own, qb = take(11)
+    dqt = acc
+    gsq, gso, gsg, gsd, grq, gro, grg, grd = take(8)
+    xq, xo, xg, xd = crosses
+    nsum_t, nsum_c, nsum_f, cot_v = take(4)
+    w_ss, w_rs, kv_ss, kv_rs, id_ss, id_rs, rs_ss, rs_rs, ag_ss, ag_rs = take(10)
+    kvg_ss, kvg_rs, gr_ss, gr_rs, x_ss, x_rs, n_ss, n_rs, loc_sem = take(9)
+    own_sem = take(1)[0]
+    if adam:
+        stages, sends = take(4), take(4)
+        m_ss, m_rs, in_sem = take(3)
 
     z, x, t = lax.axis_index("fsdp"), lax.axis_index("context"), lax.axis_index("tensor")
     core, yy = t % 2, t // 2
@@ -100,10 +118,19 @@
     for d in range(1, NT4):
         pl.semaphore_signal(barrier, inc=1, device_id={"tensor": (t + d) % NT4}, device_id_type=MESH)
 
+    def moment_load(k, i):
+        return pltpu.make_async_copy(
+            moments[2 * k + i].at[0], stages[k].at[i], in_sem.at[k, i]
+        )
+
     cot_copy = pltpu.make_async_copy(
         cot.at[:, pl.ds(pl.multiple_of(t * TS, TS), TS), :], cot_v, loc_sem.at[0]
     )
     cot_copy.start()
+    if adam:
+        for k in range(4):
+            for i in range(2):
+                moment_load(k, i).start()
 
     def own_rows(index):
         return pl.ds(pl.multiple_of(index * DB, DB), DB)
@@ -119,8 +146,8 @@
 
     wq[own_rows(z), :] = jnp.concatenate(
         [
-            pad_cols(wq_in[:, 0, :], 0, QW - C),
-            jnp.concatenate([wq_in[:, 1, :], wq_in[:, 2, :]], axis=1),
+            pad_cols(wq_in[0], 0, QW - C),
+            jnp.concatenate([wq_in[1], wq_in[2]], axis=1),
         ],
         axis=1,
     ).astype(BF16)
@@ -168,7 +195,7 @@
 
     wo_t = jnp.transpose(wo_in[...])
     wo[own_rows(z), :] = pad_cols(wo_t, HD, 0).astype(BF16)
-    wd[own_rows(z), :] = jnp.transpose(wd_in[...]).astype(BF16)
+    wd[own_rows(z), :] = wd_in[...].astype(BF16)
     wg[own_rows(z), 0:F] = wg_in[:, 0, :].astype(BF16)
     wg[own_rows(z), F : 2 * F] = wg_in[:, 1, :].astype(BF16)
 
@@ -440,27 +467,43 @@
         total = source[own_rows(z), :].astype(F32)
         for d in range(1, NF):
             total = total + landing[d - 1].astype(F32)
-        crossing[x] = total.astype(BF16)
+        source[own_rows(z), :] = total.astype(BF16)
         for d in range(1, NC):
-            cross_copy(slot, crossing, d).start()
-
-    def cross_copy(slot, crossing, d):
+            cross_copy(slot, source, crossing, d).start()
+        own_copy(slot, source).start()
+
+    def cross_copy(slot, source, crossing, d):
         return remote(
-            crossing.at[x], crossing.at[x],
+            source.at[own_rows(z), :], crossing.at[d - 1],
             x_ss.at[slot, d - 1], x_rs.at[slot, d - 1], "context", (x + d) % NC,
         )
 
-    def reduce_finish(slot, source, landing, crossing, out):
+    def own_copy(slot, source):
+        return pltpu.make_async_copy(
+            source.at[own_rows(z), :], own_out[slot], own_sem.at[slot]
+        )
+
+    def reduce_finish(slot, source, landing, crossing):
         for d in range(1, NC):
-            cross_copy(slot, crossing, d).wait_recv()
-        total = crossing[0].astype(F32)
-        for i in range(1, NC):
-            total = total + crossing[i].astype(F32)
-        out[...] = total
-        for d in range(1, NC):
-            cross_copy(slot, crossing, d).wait_send()
+            cross_copy(slot, source, crossing, d).wait()
+        own_copy(slot, source).wait()
         for d in range(1, NF):
             reduce_copy(slot, source, landing, d).wait_send()
+
+    def moment_copy(k):
+        return remote(
+            sends[k], lands[k], m_ss.at[k], m_rs.at[k], "context", (x + 1) % NC
+        )
+
+    def moment_send(k):
+        for i in range(2):
+            moment_load(k, i).wait()
+            if k == 2:
+                for j in range(2):
+                    sends[k][i, :, j * F : (j + 1) * F] = stages[k][i, :, j, :].astype(BF16)
+            else:
+                sends[k][i] = stages[k][i].astype(BF16)
+        moment_copy(k).start()
 
     def norm_copy(buffer, axis, me, count, base, d):
         return remote(
@@ -554,7 +597,7 @@
             lax.fori_loop(1, NC, far, 0)
         parts = block(0)
         for k in range(3):
-            kv_own[s, :, k * 128 : (k + 1) * 128] = parts[k]
+            kv_own[s, :, k * 128 : (k + 1) * 128] = parts[k].astype(BF16)
         grad = jnp.transpose(dqt[...]) * scale
         q0, q1 = rotate_pair(grad, slice(0, T), -1.0)
         qb[s, :, 0:128] = q0.astype(BF16)
@@ -566,7 +609,7 @@
 
         def column(k):
             cols = slice(k * 128, (k + 1) * 128)
-            total = kv_own[s, :, cols]
+            total = kv_own[s, :, cols].astype(F32)
             for d in range(1, NC):
                 total = total + kvg_r[d - 1, s, :, cols].astype(F32)
             return total
@@ -582,13 +625,20 @@
         return mm(qb[s, rows, :], wq[...], NT)
 
     def input_out(s):
-        input_grad[s] = n1[s] + rs_finish(3, s)
+        n1[s] = n1[s] + rs_finish(3, s)
+        input_copy(s).start()
+
+    def input_copy(s):
+        return pltpu.make_async_copy(n1.at[s], input_grad.at[s], loc_sem.at[1 + s])
 
     seqs = range(S)
     R = S * T
 
     for s in seqs:
         project(s)
+    if adam:
+        for k in (2, 0, 3, 1):
+            moment_send(k)
     wait_recv(wo_copies)
     wg_copies = gather(wg, 2)
     wd_copies = gather(wd, 3)
@@ -662,11 +712,13 @@
     for s in seqs:
         input_out(s)
     reduce_middle(0, gsq, grq, xq)
-    reduce_finish(3, gsd, grd, xd, gd_out)
-    reduce_finish(2, gsg, grg, xg, gg_out)
-    reduce_finish(1, gso, gro, xo, go_out)
-    reduce_finish(0, gsq, grq, xq, gq_out)
-
+    reduce_finish(3, gsd, grd, xd)
+    reduce_finish(2, gsg, grg, xg)
+    reduce_finish(1, gso, gro, xo)
+    reduce_finish(0, gsq, grq, xq)
+
+    for s in seqs:
+        input_copy(s).wait()
     for copies in (wq_copies, wo_copies, wg_copies, wd_copies, id_copies):
         wait_send(copies)
     for s in seqs:
@@ -682,14 +734,192 @@
     for level in range(3):
         for d in range(1, norm_levels[level][3]):
             norm_copy(*norm_levels[level], d).wait_send()
-
-
-def run_layer(tokens, cotangent, segment_ids, weights, norm_gains, norm_biases, cosine, sine_rows):
-    qkv_weight, out_weight, gate_up_weight, down_weight = weights
+    if adam:
+        for k in range(4):
+            moment_copy(k).wait()
+
+
+def finish_kernel(dims, *refs):
+    S, T, D, C, F, NF, NC, NT4 = dims
+    DB, QW = D // NF, 256
+    refs = list(refs)
+
+    def take(count):
+        taken, refs[:] = refs[:count], refs[count:]
+        return taken
+
+    owner, norm_sums, norm_m, norm_v = take(4)
+    layer_in, input_in = take(2)
+    own_in, cross_in, masters_in, moments_in, lands_in = take(4), take(4), take(4), take(8), take(4)
+    layer_out, input_out = take(2)
+    grads_out, states_out = take(4), take(4)
+    norm_out, norm_state, norm_flat, updates = take(4)
+    layer_v, input_v = take(2)
+    own_g, cross_g, masters, lands = take(4), take(4), take(4), take(4)
+    states, grads, flats = take(4), take(4), take(4)
+    row_a, row_b, in_sem, out_sem, pass_sem = take(5)
+    z, x, t = lax.axis_index("fsdp"), lax.axis_index("context"), lax.axis_index("tensor")
+    order = (2, 3, 1, 0)
+
+    def loads(k):
+        pairs = [
+            (own_in[k], own_g[k]), (cross_in[k], cross_g[k]), (masters_in[k], masters[k]),
+            (lands_in[k], lands[k]),
+            (moments_in[2 * k].at[0], states[k].at[0]),
+            (moments_in[2 * k + 1].at[0], states[k].at[1]),
+        ]
+        return [
+            pltpu.make_async_copy(src, dst, in_sem.at[k, i]) for i, (src, dst) in enumerate(pairs)
+        ]
+
+    def passing(k, stage):
+        src, mid, dst = ((layer_in, layer_v, layer_out), (input_in, input_v, input_out))[k]
+        if stage == 0:
+            return pltpu.make_async_copy(src, mid, pass_sem.at[k, 0])
+        return pltpu.make_async_copy(mid, dst, pass_sem.at[k, 1])
+
+    for k in order:
+        for c in loads(k):
+            c.start()
+    for k in range(2):
+        passing(k, 0).start()
+
+    def adam_parts(g, m, v, w, decay):
+        m_new = BETA_ONE * m + (1.0 - BETA_ONE) * g
+        v_new = BETA_TWO * v + (1.0 - BETA_TWO) * g * g
+        corrected = m_new / (1.0 - BETA_ONE**ADAM_STEP)
+        scaled = v_new / (1.0 - BETA_TWO**ADAM_STEP)
+        step = corrected / (jnp.sqrt(scaled) + ADAM_EPS)
+        if decay:
+            step = step + decay * w
+        return m_new, v_new, -RATE * step
+
+    def rows_to_flat(flat, count, width):
+        block = math.lcm(width, 128)
+        period, lines = block // width, block // 128
+        many = count // period
+        halves = (row_a, row_b)
+        for line in range(lines):
+            parts, at = [], line * 128
+            while at < (line + 1) * 128:
+                row, column = divmod(at, width)
+                half, lane = divmod(column, 128)
+                length = min((line + 1) * 128 - at, width - column, 128 - lane)
+                rows = halves[half][pl.ds(row, many, stride=period), :]
+                parts.append(rows[:, lane : lane + length])
+                at += length
+            whole = parts[0] if len(parts) == 1 else jnp.concatenate(parts, axis=1)
+            flat[pl.ds(line, many, stride=lines), :] = whole
+
+    def to_rows(values, rows):
+        width = values.shape[1]
+        for half, place in enumerate((row_a, row_b)):
+            part = values[:, half * 128 : min(width, (half + 1) * 128)]
+            if part.shape[1] == 0:
+                continue
+            if part.shape[1] < 128:
+                rest = jnp.zeros((part.shape[0], 128 - part.shape[1]), F32)
+                part = jnp.concatenate([part, rest], axis=1)
+            place[rows, :] = part
+
+    sizes = (DB * 3 * C, C * DB, DB * 2 * F, F * DB)
+
+    def out_copies(k):
+        first = sum(sizes[:k])
+        return (
+            pltpu.make_async_copy(grads[k], grads_out[k], out_sem.at[k, 0]),
+            pltpu.make_async_copy(states[k], states_out[k], out_sem.at[k, 1]),
+            pltpu.make_async_copy(
+                flats[k].reshape(1, sizes[k]),
+                updates.at[0, :, pl.ds(first, sizes[k])],
+                out_sem.at[k, 2],
+            ),
+        )
+
+    for k in order:
+        for c in loads(k):
+            c.wait()
+        own = own_g[k][...].astype(F32)
+        if NC == 2:
+            total = own + cross_g[k][0].astype(F32)
+        else:
+            total = jnp.zeros_like(own)
+            for i in range(NC):
+                other = cross_g[k][jnp.maximum((x - i + NC) % NC, 1) - 1].astype(F32)
+                total = total + jnp.where(x == i, own, other)
+        if k == 0:
+            parts = [total[:, 0:C], total[:, QW : QW + C], total[:, QW + C : QW + 2 * C]]
+        elif k == 1:
+            parts = [jnp.transpose(total)[HD : HD + C, :]]
+        elif k == 2:
+            parts = [total[:, 0:F], total[:, F : 2 * F]]
+        else:
+            parts = [total]
+        mine = owner[0:1, k : k + 1] == x
+        for j, g in enumerate(parts):
+            at = (j,) if k == 0 else (slice(None), j) if k == 2 else (slice(None),)
+            land_at = (slice(None), slice(j * F, (j + 1) * F)) if k == 2 else at
+            grads[k][at] = g
+            kept = [
+                jnp.where(
+                    mine, states[k][(i, *at)].astype(BF16).astype(F32),
+                    lands[k][(i, *land_at)].astype(F32),
+                )
+                for i in range(2)
+            ]
+            m_new, v_new, step = adam_parts(g, *kept, masters[k][at], DECAY)
+            states[k][(0, *at)] = m_new
+            states[k][(1, *at)] = v_new
+            if k == 0:
+                to_rows(step, pl.ds(j, DB, stride=3))
+            elif k == 1:
+                to_rows(step, pl.ds(0, C))
+            elif k == 2:
+                for c in range(F // 128):
+                    flats[2][pl.ds(j * (F // 128) + c, DB, stride=2 * F // 128), :] = step[
+                        :, c * 128 : (c + 1) * 128
+                    ]
+            else:
+                to_rows(jnp.transpose(step), pl.ds(0, F))
+        if k != 2:
+            rows_to_flat(flats[k], (3 * DB, C, 0, F)[k], (C, DB, 0, DB)[k])
+        for c in out_copies(k):
+            c.start()
+        if k == 2:
+            for i in range(2):
+                passing(i, 0).wait()
+                passing(i, 1).start()
+
+    g = norm_sums[0:4, :]
+    m_new, v_new, step = adam_parts(g, norm_m[...], norm_v[...], None, 0.0)
+    norm_out[...] = g
+    norm_state[0] = m_new
+    norm_state[1] = v_new
+    count = 4 * D // (NF * NT4)
+    per_row = D // count
+    place = z * NT4 + t
+    row = lax.broadcasted_iota(jnp.int32, (4, count), 0)
+    chosen = jnp.zeros((4, count), F32)
+    for c in range(per_row):
+        hit = row * per_row + c == place
+        chosen = chosen + jnp.where(hit, step[:, c * count : (c + 1) * count], 0.0)
+    norm_flat[...] = jnp.sum(chosen, axis=0, keepdims=True)
+    for k in order:
+        for c in out_copies(k):
+            c.wait()
+    for k in range(2):
+        passing(k, 1).wait()
+
+
+def run_layer(
+    tokens, cotangent, segment_ids, owner, weights, norm_gains, norm_biases, moments,
+    norm_moments, cosine, sine_rows,
+):
     S, T, D = tokens.shape
-    C, F = qkv_weight.shape[2], gate_up_weight.shape[2]
+    C, F = weights[0].shape[2], weights[2].shape[2]
     NF, NC, NT4 = lax.axis_size("fsdp"), lax.axis_size("context"), lax.axis_size("tensor")
     TS, DB, KW, W = T // NT4, D // NF, 384, 640
+    adam = NC == 2
     assert NT4 == 4 and C == 192
     vmem = pl.BlockSpec(memory_space=pltpu.VMEM)
     far = pl.BlockSpec(memory_space=pl.ANY)
@@ -705,59 +935,106 @@
         VM((S, 4, TS, D), BF16), VM((S, 4, TS, D), BF16), VM((S, 4, TS, D), BF16),
         VM((S, T, F), BF16), VM((S, T, 2 * F), BF16),
         VM((S, TS, D), F32), VM((S, TS, D), F32), VM((S, TS, 128), F32),
-        VM((S, T, 256), BF16), VM((S, 8, T), F32), VM((256, T), F32),
+        VM((S, T, 256), BF16), VM((S, 8, T), F32),
         VM((T, 256), F32), VM((T, 256), F32), VM((min(NX, 2), S, T, KW), BF16), VM((NX, S, T, KW), BF16),
-        VM((S, T, KW), F32), VM((S, T, W), BF16),
+        VM((S, T, KW), BF16), VM((S, T, W), BF16),
         VM((D, W), BF16), VM((D, 256), BF16), VM((D, 2 * F), BF16), VM((D, F), BF16),
         VM((NF - 1, DB, W), BF16), VM((NF - 1, DB, 256), BF16), VM((NF - 1, DB, 2 * F), BF16),
         VM((NF - 1, DB, F), BF16),
-        VM((NC, DB, W), BF16), VM((NC, DB, 256), BF16), VM((NC, DB, 2 * F), BF16), VM((NC, DB, F), BF16),
         VM((NT4, 8, D), F32), VM((NC, 8, D), F32), VM((NF, 8, D), F32), VM((S, TS, D), BF16),
         DMA((4, NF - 1)), DMA((4, NF - 1)), DMA((S, NX)), DMA((S, NX)), DMA((NX,)), DMA((NX,)),
         DMA((4, S, 3)), DMA((4, S, 3)), DMA((3, S, 3)), DMA((3, S, 3)),
         DMA((NX, S)), DMA((NX, S)), DMA((4, NF - 1)), DMA((4, NF - 1)), DMA((4, NX)), DMA((4, NX)),
-        DMA((NT4 + NC + NF,)), DMA((NT4 + NC + NF,)), DMA((1,)),
+        DMA((NT4 + NC + NF,)), DMA((NT4 + NC + NF,)), DMA((1 + S,)), DMA((4,)),
     ]
-    outs = (
+    shapes = ((3, DB, C), (C, DB), (DB, 2, F), (DB, F))
+    flat_shapes = ((DB, W), (DB, 256), (DB, 2 * F), (DB, F))
+    low_shapes = ((2, 3, DB, C), (2, C, DB), (2, DB, 2 * F), (2, DB, F))
+    dims = (S, T, D, C, F, NF, NC, NT4)
+    outs = [
         jax.ShapeDtypeStruct((S, TS, D), BF16),
         jax.ShapeDtypeStruct((S, TS, D), F32),
-        jax.ShapeDtypeStruct((DB, W), F32),
-        jax.ShapeDtypeStruct((DB, 256), F32),
-        jax.ShapeDtypeStruct((DB, 2 * F), F32),
-        jax.ShapeDtypeStruct((DB, F), F32),
+        *(jax.ShapeDtypeStruct(shape, BF16) for shape in flat_shapes),
+        *(jax.ShapeDtypeStruct((NX, *shape), BF16) for shape in flat_shapes),
         jax.ShapeDtypeStruct((8, D), F32),
-    )
-    return pl.pallas_call(
-        functools.partial(layer_kernel, (S, T, D, C, F, NF, NC, NT4)),
+    ]
+    out_specs = [vmem] + [far] * 9 + [vmem]
+    args = [
+        tokens, cotangent, segment_ids, *weights, norm_gains, norm_biases, cosine, sine_rows,
+    ]
+    in_specs = [vmem, far] + [vmem] * 9
+    flat_moments = [m for pair in moments for m in pair]
+    if adam:
+        outs += [jax.ShapeDtypeStruct(shape, BF16) for shape in low_shapes]
+        out_specs += [far] * 4
+        args += flat_moments
+        in_specs += [far] * 8
+        scratch += [VM((2, *shape), F32) for shape in shapes]
+        scratch += [VM(shape, BF16) for shape in low_shapes]
+        scratch += [DMA((4,)), DMA((4,)), DMA((4, 2))]
+    results = pl.pallas_call(
+        functools.partial(layer_kernel, dims),
         out_shape=outs,
-        in_specs=[vmem, far] + [vmem] * 9,
-        out_specs=[vmem] * len(outs),
+        in_specs=in_specs,
+        out_specs=out_specs,
         scratch_shapes=scratch,
         compiler_params=pltpu.CompilerParams(
             collective_id=0, has_side_effects=True, vmem_limit_bytes=67043328
         ),
         name="layer",
+    )(*args)
+    layer_out, input_grad = results[:2]
+    own_grads, cross_grads, norm_sums = results[2:6], results[6:10], results[10]
+    if adam:
+        lands = results[11:]
+    else:
+        lands = []
+        for k in range(4):
+            pair = jnp.concatenate(moments[k], axis=0).astype(BF16).reshape(low_shapes[k])
+            lands.append(from_root(pair, "context", owner[k]))
+        owner = jnp.full_like(owner, -1)
+
+    total = sum(math.prod(shape) for shape in shapes)
+    count = 4 * D // (NF * NT4)
+    out_shape = [
+        jax.ShapeDtypeStruct((S, TS, D), BF16),
+        jax.ShapeDtypeStruct((S, TS, D), F32),
+        *(jax.ShapeDtypeStruct(shape, F32) for shape in shapes),
+        *(jax.ShapeDtypeStruct((2, *shape), F32) for shape in shapes),
+        jax.ShapeDtypeStruct((4, D), F32),
+        jax.ShapeDtypeStruct((2, 4, D), F32),
+        jax.ShapeDtypeStruct((1, count), F32),
+        jax.ShapeDtypeStruct((1, 1, total + count), F32),
+    ]
+    rows = max(3 * DB, F)
+    return pl.pallas_call(
+        functools.partial(finish_kernel, dims),
+        out_shape=out_shape,
+        in_specs=[vmem] * 4 + [far] * 26,
+        out_specs=[far] * 10 + [vmem] * 3 + [far],
+        scratch_shapes=[
+            VM((S, TS, D), BF16), VM((S, TS, D), F32),
+            *(VM(shape, BF16) for shape in flat_shapes),
+            *(VM((NX, *shape), BF16) for shape in flat_shapes),
+            *(VM(shape, F32) for shape in shapes),
+            *(VM(shape, BF16) for shape in low_shapes),
+            *(VM((2, *shape), F32) for shape in shapes),
+            *(VM(shape, F32) for shape in shapes),
+            *(VM((math.prod(shape) // 128, 128), F32) for shape in shapes),
+            VM((rows, 128), F32), VM((rows, 128), F32),
+            DMA((4, 6)), DMA((4, 3)), DMA((2, 2)),
+        ],
+        compiler_params=pltpu.CompilerParams(vmem_limit_bytes=67043328),
+        name="finish",
     )(
-        tokens, cotangent, segment_ids, qkv_weight, out_weight, gate_up_weight, down_weight,
-        norm_gains, norm_biases, cosine, sine_rows,
+        owner.reshape(1, 4), norm_sums, *norm_moments, layer_out, input_grad, *own_grads,
+        *cross_grads, *weights, *flat_moments, *lands,
     )
 
 
 def from_root(block, axis, owner):
     block = jnp.where(lax.axis_index(axis) == owner, block, jnp.zeros_like(block))
     return lax.psum(block, axis)
-
-
-def moment_pair(gradient, moment, square):
-    moment_new = BETA_ONE * moment + (1.0 - BETA_ONE) * gradient
-    square_new = BETA_TWO * square + (1.0 - BETA_TWO) * gradient * gradient
-    return jnp.stack([moment_new, square_new])
-
-
-def step_of(pair_new, master, decay_rate):
-    corrected = pair_new[0] / (1.0 - BETA_ONE**ADAM_STEP)
-    scaled = pair_new[1] / (1.0 - BETA_TWO**ADAM_STEP)
-    return -RATE * (corrected / (jnp.sqrt(scaled) + ADAM_EPS) + decay_rate * master)
 
 
 def shards(
@@ -765,22 +1042,11 @@
     norm_gains, norm_biases, qkv_moment, qkv_square, out_moment, out_square, gate_moment,
     gate_square, down_moment, down_square, norm_moment, norm_square,
 ):
-    seqs_here, tok_here, model_width = tokens.shape
-    head_cols = qkv_weight.shape[2]
-    hidden_here = gate_up_weight.shape[2]
-    tensor_size, fsdp_size = lax.axis_size("tensor"), lax.axis_size("fsdp")
-    masters = (qkv_weight, out_weight, gate_up_weight, down_weight)
+    tok_here = tokens.shape[1]
     moments = (
         (qkv_moment, qkv_square), (out_moment, out_square),
         (gate_moment, gate_square), (down_moment, down_square),
     )
-    owned = [
-        [
-            from_root(slot[0].astype(BF16), "context", owner[k]).astype(F32)
-            for slot in moments[k]
-        ]
-        for k in range(4)
-    ]
     positions = (
         lax.axis_index("context") * tok_here + jnp.arange(tok_here, dtype=jnp.int32)
     ).astype(F32)
@@ -790,30 +1056,32 @@
     cosine = jnp.concatenate([cosine] * 4, axis=1)
     sine_rows = jnp.concatenate([-sine_rows, sine_rows] * 2, axis=1)
 
-    layer_out, input_grad, grad_q, grad_o, grad_g, grad_d, norm_sums = run_layer(
-        tokens, cotangent, segment_ids, masters, norm_gains, norm_biases, cosine, sine_rows
+    columns_last = (0, 2, 1, 3)
+    weights = (
+        jnp.transpose(qkv_weight, (1, 0, 2)), out_weight, gate_up_weight, jnp.transpose(down_weight),
     )
-    rows = qkv_weight.shape[0]
-    weight_grads = (
-        jnp.concatenate([grad_q[:, :head_cols], grad_q[:, 256:]], axis=1).reshape(rows, 3, head_cols),
-        jnp.transpose(grad_o[:, HD:]),
-        grad_g.reshape(rows, 2, hidden_here),
-        jnp.transpose(grad_d),
+    turned = (
+        [jnp.transpose(m, columns_last) for m in moments[0]],
+        moments[1],
+        moments[2],
+        [jnp.transpose(m, (0, 2, 1)) for m in moments[3]],
     )
-    norm_grad = norm_sums[:4]
-    new_pairs = [moment_pair(weight_grads[k], owned[k][0], owned[k][1]) for k in range(4)]
-    new_steps = [step_of(new_pairs[k], masters[k], DECAY) for k in range(4)]
-    norm_master = jnp.concatenate([norm_gains, norm_biases], axis=0)
-    norm_state = moment_pair(norm_grad, norm_moment, norm_square)
-    norm_step = step_of(norm_state, norm_master, 0.0).reshape(-1)
-    piece = norm_step.shape[0] // (fsdp_size * tensor_size)
-    start = (lax.axis_index("fsdp") * tensor_size + lax.axis_index("tensor")) * piece
-    norm_piece = lax.dynamic_slice_in_dim(norm_step, start, piece, 0)
-    weight_updates = jnp.concatenate(
-        [value.reshape(-1) for value in new_steps] + [norm_piece], axis=0
-    ).reshape(1, 1, -1)
+    results = run_layer(
+        tokens, cotangent, segment_ids, owner, weights, norm_gains, norm_biases, turned,
+        (norm_moment, norm_square), cosine, sine_rows,
+    )
+    layer_out, input_grad, grad_q, grad_o, grad_g, grad_d = results[:6]
+    state_q, state_o, state_g, state_d = results[6:10]
+    norm_grad, norm_state, piece, weight_updates = results[10:]
+    weight_updates = lax.dynamic_update_slice(
+        weight_updates, piece[None], (0, 0, weight_updates.shape[2] - piece.shape[1])
+    )
     return (
-        layer_out, input_grad, *weight_grads, norm_grad, *new_pairs, norm_state, weight_updates
+        layer_out, input_grad,
+        jnp.transpose(grad_q, (1, 0, 2)), grad_o, grad_g, jnp.transpose(grad_d),
+        norm_grad,
+        jnp.transpose(state_q, columns_last), state_o, state_g, jnp.transpose(state_d, (0, 2, 1)),
+        norm_state, weight_updates,
     )
 
 

time: 371 us -> 300 us (0.81)
  local copies, waits for them, and re-layouts: 44.7 us -> 1.17 us
  other arithmetic: 24.2 us -> 2.27 us
  between operations: 17.6 us -> 1.12 us
  Pallas kernels: 277 us -> 291 us
    unnamed x87 -> x0, local copies, waits for them, and re-layouts: 19.4 us -> none
    reshape x7 -> x0, local copies, waits for them, and re-layouts: 18 us -> none  [the longest x1 12 us: shards(): weight_updates = jnp.concatenate([value.reshape(-1) for value in new_step...]
    pallas_call x1 -> x2, Pallas kernels: 277 us -> 291 us  [the longest x1 276 us: run_layer(): pl.pallas_call(functools.partial(layer_kernel, dims), out_shape=outs, in_...]
    mul x5 -> x0, other arithmetic: 13 us -> none  [step_of(): -RATE * (corrected / (jnp.sqrt(scaled) + ADAM_EPS) + decay_rate * master)]
    select_n x4 -> x0, other arithmetic: 4.38 us -> none  [from_root(): jnp.where(lax.axis_index(axis) == owner, block, jnp.zeros_like(block))]
    another operation x6 -> x0, other arithmetic: 4.36 us -> none  [moment_pair(): return jnp.stack([moment_new, square_new])]
  transfers between devices with their start and end apart: 1 -> 0, of which waited for: 0 -> 0; matrix products, arithmetic and copies ran while one was open for 4% -> 0% of each run, Pallas kernels for 76% -> 0%
where the time goes in v2:
time: 300 us; the launch traced here: 295 us
  Pallas kernels  291 us (97%)
    pallas_call x1, Pallas kernels, run_layer(): pl.pallas_call(functools.partial(layer_kernel, dims), out_shape=outs, in_...  276 us
    pallas_call x1, Pallas kernels, run_layer(): pl.pallas_call(functools.partial(finish_kernel, dims), out_shape=out_shap...  14.6 us

profile of v2, /device:TPU:26, one launch (start us, length us, event | category | flops | bytes accessed | tf_op | source)
XLA Modules:
  0.0 295.1 jit_solution(16322405492072085192)
XLA Ops:
  0.7 1.0 fusion
  1.7 1.3 pad_maximum_fusion
  2.9 275.9 %layer.1 = (bf16[2,128,768]{2,1,0:T(8,128)(2,1)}, f32[2,128,768]{2,1,0:T(8,128)}, bf16[192,640]{1,0:T(8,128)(2,1)}, bf16[192,256]{1,0:T(8,128)(2,1)}, bf16[192,1...) custom-call(bf16[2,512,768]{2,1,0:T(8,128)(2,1)} %refs_0_.1, ...), custom_call_target="tpu_custom_call" | custom-call | tf_op jit(solution)/shard_map/layer/pallas_call | solution.py:975
  278.9 14.6 %finish.1 = (bf16[2,128,768]{2,1,0:T(8,128)(2,1)}, f32[2,128,768]{2,1,0:T(8,128)}, f32[3,192,192]{2,1,0:T(8,128)}, f32[192,192]{1,0:T(8,128)}, f32[192,2,768]{2,...) custom-call(s32[1,4]{1,0:T(1,128)} %bitcast.25, ...), custom_call_target="tpu_custom_call" | custom-call | tf_op jit(solution)/shard_map/finish/pallas_call | solution.py:1010
  293.5 1.2 bitcast_dynamic-update-slice_fusion
  (2 shorter events, 0.0 us)

commit v3 on v2

--- a/solution.py
+++ b/solution.py
@@ -64,10 +64,12 @@
 
 def layer_kernel(dims, *refs):
     S, T, D, C, F, NF, NC, NT4 = dims
-    adam = NC == 2
-    refs = list(refs)
     TS = T // NT4
     DB = D // NF
+    adam = NC == 2
+    pair = NC == 2
+    HB = DB // 2
+    refs = list(refs)
     QW, KW = 256, 384
     H = C // HD
     KS = min(max(NC - 1, 1), 2)
@@ -80,7 +82,7 @@
     if adam:
         moments = take(8)
     layer_out, input_grad = take(2)
-    own_out, crosses = take(4), take(4)
+    own_out, crosses = take(5), take(5)
     norm_out = take(1)[0]
     if adam:
         lands = take(4)
@@ -88,12 +90,11 @@
     rsend, rsb, rs2, rs2r, ag1, ag2, ag3, hid, gb = take(9)
     n1, unit1, inv1, datt, dlt, dk, dv, kvg_s, kvg_r, kv_own, qb = take(11)
     dqt = acc
-    gsq, gso, gsg, gsd, grq, gro, grg, grd = take(8)
-    xq, xo, xg, xd = crosses
+    sources, landings, meets = take(5), take(5), take(2)
     nsum_t, nsum_c, nsum_f, cot_v = take(4)
     w_ss, w_rs, kv_ss, kv_rs, id_ss, id_rs, rs_ss, rs_rs, ag_ss, ag_rs = take(10)
     kvg_ss, kvg_rs, gr_ss, gr_rs, x_ss, x_rs, n_ss, n_rs, loc_sem = take(9)
-    own_sem = take(1)[0]
+    own_sem, f_ss, f_rs, h_ss, h_rs, l_ss, l_rs = take(7)
     if adam:
         stages, sends = take(4), take(4)
         m_ss, m_rs, in_sem = take(3)
@@ -154,18 +155,39 @@
 
     pl.semaphore_wait(barrier, NF - 1 + NC - 1 + NT4 - 1)
 
-    def gather(buffer, slot):
-        copies = []
+    def half_rows(block, half):
+        return pl.ds(pl.multiple_of(block * DB + half * HB, HB), HB)
+
+    def fetch_copy(buffer, slot, d):
+        rows = half_rows(z, x) if pair else own_rows(z)
+        return remote(
+            buffer.at[rows, :], buffer.at[rows, :],
+            w_ss.at[slot, d - 1], w_rs.at[slot, d - 1], "fsdp", (z + d) % NF,
+        )
+
+    def hand_copy(buffer, slot, d):
+        rows = half_rows((z + NF - d) % NF, x)
+        return remote(
+            buffer.at[rows, :], buffer.at[rows, :],
+            f_ss.at[slot, d - 1], f_rs.at[slot, d - 1], "context", 1 - x,
+        )
+
+    def gather_start(slot):
         for d in range(1, NF):
-            copies.append(
-                remote(
-                    buffer.at[own_rows(z), :], buffer.at[own_rows(z), :],
-                    w_ss.at[slot, d - 1], w_rs.at[slot, d - 1], "fsdp", (z + d) % NF,
-                )
-            )
-        for c in copies:
-            c.start()
-        return copies
+            fetch_copy(gathered[slot], slot, d).start()
+
+    def gather_hand(slot):
+        for d in range(1, NF):
+            fetch_copy(gathered[slot], slot, d).wait_recv()
+            if pair:
+                hand_copy(gathered[slot], slot, d).start()
+
+    def gather_finish(slot):
+        if pair:
+            for d in range(1, NF):
+                hand_copy(gathered[slot], slot, d).wait_recv()
+
+    gathered = (wq, wo, wg, wd)
 
     def wait_recv(copies):
         for c in copies:
@@ -175,7 +197,7 @@
         for c in copies:
             c.wait_send()
 
-    wq_copies = gather(wq, 0)
+    gather_start(0)
 
     ids_all[x] = ids_in[...]
     id_copies = []
@@ -199,8 +221,11 @@
     wg[own_rows(z), 0:F] = wg_in[:, 0, :].astype(BF16)
     wg[own_rows(z), F : 2 * F] = wg_in[:, 1, :].astype(BF16)
 
-    wait_recv(wq_copies)
-    wo_copies = gather(wo, 1)
+    gather_hand(0)
+    gather_start(1)
+    gather_start(2)
+    gather_start(3)
+    gather_finish(0)
 
     def rotate_pair(values, rows, sign):
         cosine, sine_rows = cos_t[rows, :], sin_t[rows, :] * sign
@@ -450,52 +475,101 @@
 
         lax.fori_loop(0, D // 128, tile, 0)
 
-    def reduce_start(slot, source, landing):
+    def reduce_copy(slot, d):
+        to = (z + d) % NF
+        rows = half_rows(to, x) if two_level(slot) else own_rows(to)
+        return remote(
+            sources[slot].at[rows, :], landings[slot].at[d - 1],
+            gr_ss.at[slot, d - 1], gr_rs.at[slot, d - 1], "fsdp", to,
+        )
+
+    def two_level(slot):
+        return pair and slot in (2, 3)
+
+    def meet_copy(slot, block):
+        return remote(
+            sources[slot].at[half_rows(block, 1 - x), :], meets[slot - 2].at[block],
+            h_ss.at[slot - 2, block], h_rs.at[slot - 2, block], "context", 1 - x,
+        )
+
+    def reduce_start(slot):
         for d in range(1, NF):
-            reduce_copy(slot, source, landing, d).start()
-
-    def reduce_copy(slot, source, landing, d):
-        to = (z + d) % NF
+            if two_level(slot):
+                meet_copy(slot, (z + d) % NF).start()
+            else:
+                reduce_copy(slot, d).start()
+        if two_level(slot):
+            meet_copy(slot, z).start()
+
+    def reduce_meet(slot):
+        if not two_level(slot):
+            return
+        for d in range(1, NF + 1):
+            block = (z + d) % NF
+            meet_copy(slot, block).wait_recv()
+            rows = half_rows(block, x)
+            sources[slot][rows, :] = (
+                sources[slot][rows, :].astype(F32) + meets[slot - 2][block].astype(F32)
+            ).astype(BF16)
+            if d < NF:
+                reduce_copy(slot, d).start()
+
+    def reduce_middle(slot):
+        rows = half_rows(z, x) if two_level(slot) else own_rows(z)
+        total = sources[slot][rows, :].astype(F32)
+        for d in range(1, NF):
+            reduce_copy(slot, d).wait_recv()
+            total = total + landings[slot][d - 1].astype(F32)
+        sources[slot][rows, :] = total.astype(BF16)
+        if two_level(slot):
+            last_copy(slot).start()
+        else:
+            for d in range(1, NC):
+                cross_copy(slot, d).start()
+        own_copy(slot).start()
+
+    def last_copy(slot):
+        place = pl.ds(pl.multiple_of(x * HB, HB), HB)
         return remote(
-            source.at[own_rows(to), :], landing.at[d - 1],
-            gr_ss.at[slot, d - 1], gr_rs.at[slot, d - 1], "fsdp", to,
-        )
-
-    def reduce_middle(slot, source, landing, crossing):
+            sources[slot].at[half_rows(z, x), :], own_out[slot].at[place, :],
+            l_ss.at[slot - 2], l_rs.at[slot - 2], "context", 1 - x,
+        )
+
+    def cross_copy(slot, d):
+        return remote(
+            sources[slot].at[own_rows(z), :], crosses[slot].at[d - 1],
+            x_ss.at[slot, d - 1], x_rs.at[slot, d - 1], "context", (x + d) % NC,
+        )
+
+    def own_copy(slot):
+        if two_level(slot):
+            place = pl.ds(pl.multiple_of(x * HB, HB), HB)
+            return pltpu.make_async_copy(
+                sources[slot].at[half_rows(z, x), :], own_out[slot].at[place, :],
+                own_sem.at[slot],
+            )
+        return pltpu.make_async_copy(
+            sources[slot].at[own_rows(z), :], own_out[slot], own_sem.at[slot]
+        )
+
+    def reduce_finish(slot):
+        if two_level(slot):
+            last_copy(slot).wait()
+            for block in range(NF):
+                meet_copy(slot, block).wait_send()
+        else:
+            for d in range(1, NC):
+                cross_copy(slot, d).wait()
+        own_copy(slot).wait()
         for d in range(1, NF):
-            reduce_copy(slot, source, landing, d).wait_recv()
-        total = source[own_rows(z), :].astype(F32)
-        for d in range(1, NF):
-            total = total + landing[d - 1].astype(F32)
-        source[own_rows(z), :] = total.astype(BF16)
-        for d in range(1, NC):
-            cross_copy(slot, source, crossing, d).start()
-        own_copy(slot, source).start()
-
-    def cross_copy(slot, source, crossing, d):
-        return remote(
-            source.at[own_rows(z), :], crossing.at[d - 1],
-            x_ss.at[slot, d - 1], x_rs.at[slot, d - 1], "context", (x + d) % NC,
-        )
-
-    def own_copy(slot, source):
-        return pltpu.make_async_copy(
-            source.at[own_rows(z), :], own_out[slot], own_sem.at[slot]
-        )
-
-    def reduce_finish(slot, source, landing, crossing):
-        for d in range(1, NC):
-            cross_copy(slot, source, crossing, d).wait()
-        own_copy(slot, source).wait()
-        for d in range(1, NF):
-            reduce_copy(slot, source, landing, d).wait_send()
+            reduce_copy(slot, d).wait_send()
 
     def moment_copy(k):
         return remote(
             sends[k], lands[k], m_ss.at[k], m_rs.at[k], "context", (x + 1) % NC
         )
 
-    def moment_send(k):
+    def moment_cast(k):
         for i in range(2):
             moment_load(k, i).wait()
             if k == 2:
@@ -503,7 +577,6 @@
                     sends[k][i, :, j * F : (j + 1) * F] = stages[k][i, :, j, :].astype(BF16)
             else:
                 sends[k][i] = stages[k][i].astype(BF16)
-        moment_copy(k).start()
 
     def norm_copy(buffer, axis, me, count, base, d):
         return remote(
@@ -636,29 +709,33 @@
 
     for s in seqs:
         project(s)
+    gather_hand(1)
     if adam:
         for k in (2, 0, 3, 1):
-            moment_send(k)
-    wait_recv(wo_copies)
-    wg_copies = gather(wg, 2)
-    wd_copies = gather(wd, 3)
-    for s in seqs:
+            moment_cast(k)
+    attend(0)
+    gather_finish(1)
+    rs_produce(0, 0, out_product)
+    for s in range(1, S):
         attend(s)
-        if s > 0:
-            rs_middle(0, s - 1)
+        rs_middle(0, s - 1)
         rs_produce(0, s, out_product)
-        if s > 0:
-            first_norm(s - 1)
+        first_norm(s - 1)
+    gather_hand(2)
     rs_middle(0, S - 1)
     first_norm(S - 1)
-    wait_recv(wg_copies)
+    gather_hand(3)
     for s in seqs:
         ag_middle(0, ag1, s)
+    gather_finish(2)
+    if adam:
+        for k in (2, 0, 3, 1):
+            moment_copy(k).start()
     for s in seqs:
         ag_finish(0, ag1, s)
         gate_up(s)
         if s == 0:
-            wait_recv(wd_copies)
+            gather_finish(3)
         rs_produce(1, s, down_product)
         if s > 0:
             rs_middle(1, s - 1)
@@ -676,16 +753,18 @@
         if s > 0:
             rs_middle(2, s - 1)
     rs_middle(2, S - 1)
-    flat_hid = hid[...].reshape(R, F)
-    weight_grad(gsd, lambda c: ag2[:, :, :, c].reshape(R, 128), flat_hid)
-    reduce_start(3, gsd, grd)
+    weight_grad(sources[3], lambda c: ag2[:, :, :, c].reshape(R, 128), hid[...].reshape(R, F))
+    reduce_start(3)
     for s in seqs:
         first_norm_back(s)
     norm_start(0)
-    weight_grad(gsg, lambda c: ag1[:, :, :, c].reshape(R, 128), gb[...].reshape(R, 2 * F))
-    reduce_start(2, gsg, grg)
+    weight_grad(
+        sources[2], lambda c: ag1[:, :, :, c].reshape(R, 128), gb[...].reshape(R, 2 * F)
+    )
+    reduce_start(2)
     for s in seqs:
         ag_middle(2, ag3, s)
+    reduce_meet(3)
     for s in seqs:
         ag_finish(2, ag3, s)
         attended_back(s)
@@ -693,34 +772,46 @@
             nsum_c[x] = norm_total(0)
             norm_start(1)
         attend_back(s)
+    reduce_meet(2)
     nsum_f[z] = norm_total(1)
     norm_start(2)
-    weight_grad(gso, lambda c: ag3[:, :, :, c].reshape(R, 128), att[...].reshape(R, 256))
-    reduce_start(1, gso, gro)
+    weight_grad(
+        sources[4], lambda c: tok[:, :, c].reshape(R, 128), qb[:, :, 0:QW].reshape(R, QW)
+    )
+    reduce_start(4)
+    weight_grad(sources[1], lambda c: ag3[:, :, :, c].reshape(R, 128), att[...].reshape(R, 256))
+    reduce_start(1)
+    reduce_middle(3)
     for s in seqs:
         keys_back(s)
+        if s == S - 1:
+            weight_grad(
+                sources[0], lambda c: tok[:, :, c].reshape(R, 128),
+                qb[:, :, QW : QW + KW].reshape(R, KW),
+            )
+            reduce_start(0)
         rs_produce(3, s, input_product)
         if s > 0:
             rs_middle(3, s - 1)
     rs_middle(3, S - 1)
-    weight_grad(gsq, lambda c: tok[:, :, c].reshape(R, 128), qb[...].reshape(R, QW + KW))
-    reduce_start(0, gsq, grq)
     norm_out[...] = norm_total(2)
-    reduce_middle(3, gsd, grd, xd)
-    reduce_middle(2, gsg, grg, xg)
-    reduce_middle(1, gso, gro, xo)
+    reduce_middle(2)
+    reduce_middle(4)
+    reduce_middle(1)
     for s in seqs:
         input_out(s)
-    reduce_middle(0, gsq, grq, xq)
-    reduce_finish(3, gsd, grd, xd)
-    reduce_finish(2, gsg, grg, xg)
-    reduce_finish(1, gso, gro, xo)
-    reduce_finish(0, gsq, grq, xq)
+    reduce_middle(0)
+    for slot in (3, 2, 4, 1, 0):
+        reduce_finish(slot)
 
     for s in seqs:
         input_copy(s).wait()
-    for copies in (wq_copies, wo_copies, wg_copies, wd_copies, id_copies):
-        wait_send(copies)
+    wait_send(id_copies)
+    for slot in range(4):
+        for d in range(1, NF):
+            fetch_copy(gathered[slot], slot, d).wait_send()
+            if pair:
+                hand_copy(gathered[slot], slot, d).wait_send()
     for s in seqs:
         for d in range(1, NC):
             kv_copy(s, d).wait_send()
@@ -741,7 +832,7 @@
 
 def finish_kernel(dims, *refs):
     S, T, D, C, F, NF, NC, NT4 = dims
-    DB, QW = D // NF, 256
+    DB = D // NF
     refs = list(refs)
 
     def take(count):
@@ -750,12 +841,13 @@
 
     owner, norm_sums, norm_m, norm_v = take(4)
     layer_in, input_in = take(2)
-    own_in, cross_in, masters_in, moments_in, lands_in = take(4), take(4), take(4), take(8), take(4)
+    own_in, cross_in, masters_in, moments_in, lands_in = take(5), take(5), take(4), take(8), take(4)
     layer_out, input_out = take(2)
     grads_out, states_out = take(4), take(4)
     norm_out, norm_state, norm_flat, updates = take(4)
     layer_v, input_v = take(2)
-    own_g, cross_g, masters, lands = take(4), take(4), take(4), take(4)
+    own_g, cross_g, masters, lands = take(5), take(5), take(4), take(4)
+    pair = NC == 2
     states, grads, flats = take(4), take(4), take(4)
     row_a, row_b, in_sem, out_sem, pass_sem = take(5)
     z, x, t = lax.axis_index("fsdp"), lax.axis_index("context"), lax.axis_index("tensor")
@@ -763,11 +855,14 @@
 
     def loads(k):
         pairs = [
-            (own_in[k], own_g[k]), (cross_in[k], cross_g[k]), (masters_in[k], masters[k]),
-            (lands_in[k], lands[k]),
+            (masters_in[k], masters[k]), (lands_in[k], lands[k]),
             (moments_in[2 * k].at[0], states[k].at[0]),
             (moments_in[2 * k + 1].at[0], states[k].at[1]),
         ]
+        for slot in ((0, 4) if k == 0 else (k,)):
+            pairs.append((own_in[slot], own_g[slot]))
+            if not (pair and slot in (2, 3)):
+                pairs.append((cross_in[slot], cross_g[slot]))
         return [
             pltpu.make_async_copy(src, dst, in_sem.at[k, i]) for i, (src, dst) in enumerate(pairs)
         ]
@@ -836,19 +931,22 @@
             ),
         )
 
+    def summed(slot):
+        own = own_g[slot][...].astype(F32)
+        if pair:
+            return own if slot in (2, 3) else own + cross_g[slot][0].astype(F32)
+        total = jnp.zeros_like(own)
+        for i in range(NC):
+            other = cross_g[slot][jnp.maximum((x - i + NC) % NC, 1) - 1].astype(F32)
+            total = total + jnp.where(x == i, own, other)
+        return total
+
     for k in order:
         for c in loads(k):
             c.wait()
-        own = own_g[k][...].astype(F32)
-        if NC == 2:
-            total = own + cross_g[k][0].astype(F32)
-        else:
-            total = jnp.zeros_like(own)
-            for i in range(NC):
-                other = cross_g[k][jnp.maximum((x - i + NC) % NC, 1) - 1].astype(F32)
-                total = total + jnp.where(x == i, own, other)
+        total = summed(k)
         if k == 0:
-            parts = [total[:, 0:C], total[:, QW : QW + C], total[:, QW + C : QW + 2 * C]]
+            parts = [summed(4)[:, 0:C], total[:, 0:C], total[:, C : 2 * C]]
         elif k == 1:
             parts = [jnp.transpose(total)[HD : HD + C, :]]
         elif k == 2:
@@ -926,6 +1024,7 @@
     VM = pltpu.VMEM
     DMA = pltpu.SemaphoreType.DMA
     NX = max(NC - 1, 1)
+    grad_columns = (KW, 256, 2 * F, F, 256)
     scratch = [
         VM((D, W), BF16), VM((D, 256), BF16), VM((D, 2 * F), BF16), VM((D, F), BF16),
         VM((NC, S, T), jnp.int32), VM((S, T, 256), BF16), VM((NC, S, T, KW), BF16),
@@ -938,17 +1037,24 @@
         VM((S, T, 256), BF16), VM((S, 8, T), F32),
         VM((T, 256), F32), VM((T, 256), F32), VM((min(NX, 2), S, T, KW), BF16), VM((NX, S, T, KW), BF16),
         VM((S, T, KW), BF16), VM((S, T, W), BF16),
-        VM((D, W), BF16), VM((D, 256), BF16), VM((D, 2 * F), BF16), VM((D, F), BF16),
-        VM((NF - 1, DB, W), BF16), VM((NF - 1, DB, 256), BF16), VM((NF - 1, DB, 2 * F), BF16),
-        VM((NF - 1, DB, F), BF16),
+        *(VM((D, columns), BF16) for columns in grad_columns),
+        *(
+            VM((NF - 1, DB // 2 if NC == 2 and slot in (2, 3) else DB, grad_columns[slot]), BF16)
+            for slot in range(5)
+        ),
+        *(
+            VM((NF, DB // 2, columns) if NC == 2 else (1, 16, 128), BF16)
+            for columns in grad_columns[2:4]
+        ),
         VM((NT4, 8, D), F32), VM((NC, 8, D), F32), VM((NF, 8, D), F32), VM((S, TS, D), BF16),
         DMA((4, NF - 1)), DMA((4, NF - 1)), DMA((S, NX)), DMA((S, NX)), DMA((NX,)), DMA((NX,)),
         DMA((4, S, 3)), DMA((4, S, 3)), DMA((3, S, 3)), DMA((3, S, 3)),
-        DMA((NX, S)), DMA((NX, S)), DMA((4, NF - 1)), DMA((4, NF - 1)), DMA((4, NX)), DMA((4, NX)),
-        DMA((NT4 + NC + NF,)), DMA((NT4 + NC + NF,)), DMA((1 + S,)), DMA((4,)),
+        DMA((NX, S)), DMA((NX, S)), DMA((5, NF - 1)), DMA((5, NF - 1)), DMA((5, NX)), DMA((5, NX)),
+        DMA((NT4 + NC + NF,)), DMA((NT4 + NC + NF,)), DMA((1 + S,)), DMA((5,)),
+        DMA((4, NF - 1)), DMA((4, NF - 1)), DMA((2, NF)), DMA((2, NF)), DMA((2,)), DMA((2,)),
     ]
     shapes = ((3, DB, C), (C, DB), (DB, 2, F), (DB, F))
-    flat_shapes = ((DB, W), (DB, 256), (DB, 2 * F), (DB, F))
+    flat_shapes = tuple((DB, columns) for columns in grad_columns)
     low_shapes = ((2, 3, DB, C), (2, C, DB), (2, DB, 2 * F), (2, DB, F))
     dims = (S, T, D, C, F, NF, NC, NT4)
     outs = [
@@ -958,7 +1064,7 @@
         *(jax.ShapeDtypeStruct((NX, *shape), BF16) for shape in flat_shapes),
         jax.ShapeDtypeStruct((8, D), F32),
     ]
-    out_specs = [vmem] + [far] * 9 + [vmem]
+    out_specs = [vmem] + [far] * 11 + [vmem]
     args = [
         tokens, cotangent, segment_ids, *weights, norm_gains, norm_biases, cosine, sine_rows,
     ]
@@ -984,9 +1090,9 @@
         name="layer",
     )(*args)
     layer_out, input_grad = results[:2]
-    own_grads, cross_grads, norm_sums = results[2:6], results[6:10], results[10]
+    own_grads, cross_grads, norm_sums = results[2:7], results[7:12], results[12]
     if adam:
-        lands = results[11:]
+        lands = results[13:]
     else:
         lands = []
         for k in range(4):
@@ -1010,7 +1116,7 @@
     return pl.pallas_call(
         functools.partial(finish_kernel, dims),
         out_shape=out_shape,
-        in_specs=[vmem] * 4 + [far] * 26,
+        in_specs=[vmem] * 4 + [far] * 28,
         out_specs=[far] * 10 + [vmem] * 3 + [far],
         scratch_shapes=[
             VM((S, TS, D), BF16), VM((S, TS, D), F32),
@@ -1022,7 +1128,7 @@
             *(VM(shape, F32) for shape in shapes),
             *(VM((math.prod(shape) // 128, 128), F32) for shape in shapes),
             VM((rows, 128), F32), VM((rows, 128), F32),
-            DMA((4, 6)), DMA((4, 3)), DMA((2, 2)),
+            DMA((4, 8)), DMA((4, 3)), DMA((2, 2)),
         ],
         compiler_params=pltpu.CompilerParams(vmem_limit_bytes=67043328),
         name="finish",

time: 300 us -> 249 us (0.83)
  Pallas kernels: 291 us -> 240 us
    pallas_call x1, Pallas kernels: 276 us -> 226 us  [run_layer(): pl.pallas_call(functools.partial(layer_kernel, dims), out_shape=outs, in_...]
where the time goes in v3:
time: 249 us; the launch traced here: 245 us
  Pallas kernels  240 us (96%)
    pallas_call x1, Pallas kernels, run_layer(): pl.pallas_call(functools.partial(layer_kernel, dims), out_shape=outs, in_...  226 us
    pallas_call x1, Pallas kernels, run_layer(): pl.pallas_call(functools.partial(finish_kernel, dims), out_shape=out_shap...  14.3 us

profile of v3, /device:TPU:26, one launch (start us, length us, event | category | flops | bytes accessed | tf_op | source)
XLA Modules:
  0.0 244.8 jit_solution(18310918524115520283)
XLA Ops:
  0.7 1.0 fusion
  1.7 1.3 pad_maximum_fusion
  2.9 226.0 %layer.1 = (bf16[2,128,768]{2,1,0:T(8,128)(2,1)}, f32[2,128,768]{2,1,0:T(8,128)}, bf16[192,384]{1,0:T(8,128)(2,1)}, bf16[192,256]{1,0:T(8,128)(2,1)}, bf16[192,1...) custom-call(bf16[2,512,768]{2,1,0:T(8,128)(2,1)} %refs_0_.1, ...), custom_call_target="tpu_custom_call" | custom-call | tf_op jit(solution)/shard_map/layer/pallas_call | solution.py:1081
  228.9 14.3 %finish.1 = (bf16[2,128,768]{2,1,0:T(8,128)(2,1)}, f32[2,128,768]{2,1,0:T(8,128)}, f32[3,192,192]{2,1,0:T(8,128)}, f32[192,192]{1,0:T(8,128)}, f32[192,2,768]{2,...) custom-call(s32[1,4]{1,0:T(1,128)} %bitcast.25, ...), custom_call_target="tpu_custom_call" | custom-call | tf_op jit(solution)/shard_map/finish/pallas_call | solution.py:1116
  243.2 1.2 bitcast_dynamic-update-slice_fusion
  (2 shorter events, 0.0 us)

commit v4 on v3

--- a/solution.py
+++ b/solution.py
@@ -26,6 +26,11 @@
 NN = (((1,), (0,)), ((), ()))
 NT = (((1,), (1,)), ((), ()))
 TN = (((0,), (0,)), ((), ()))
+
+
+FETCH_HALVES = (0, 2)
+SUM_HALVES = (2, 4)
+RELAYED = (1, 2, 3, 4)
 
 
 def mm(left, right, dims):
@@ -88,8 +93,7 @@
         lands = take(4)
     wq, wo, wg, wd, ids_all, q_ref, kv, att, tot, am, al, acc, bias_ref, vt = take(14)
     rsend, rsb, rs2, rs2r, ag1, ag2, ag3, hid, gb = take(9)
-    n1, unit1, inv1, datt, dlt, dk, dv, kvg_s, kvg_r, kv_own, qb = take(11)
-    dqt = acc
+    n1, unit1, inv1, datt, dlt, dqt, dk, dv, kvg_s, kvg_r, kv_own, qb = take(12)
     sources, landings, meets = take(5), take(5), take(2)
     nsum_t, nsum_c, nsum_f, cot_v = take(4)
     w_ss, w_rs, kv_ss, kv_rs, id_ss, id_rs, rs_ss, rs_rs, ag_ss, ag_rs = take(10)
@@ -159,7 +163,7 @@
         return pl.ds(pl.multiple_of(block * DB + half * HB, HB), HB)
 
     def fetch_copy(buffer, slot, d):
-        rows = half_rows(z, x) if pair else own_rows(z)
+        rows = half_rows(z, x) if halved(slot) else own_rows(z)
         return remote(
             buffer.at[rows, :], buffer.at[rows, :],
             w_ss.at[slot, d - 1], w_rs.at[slot, d - 1], "fsdp", (z + d) % NF,
@@ -172,6 +176,9 @@
             f_ss.at[slot, d - 1], f_rs.at[slot, d - 1], "context", 1 - x,
         )
 
+    def halved(slot):
+        return pair and slot in FETCH_HALVES
+
     def gather_start(slot):
         for d in range(1, NF):
             fetch_copy(gathered[slot], slot, d).start()
@@ -179,11 +186,11 @@
     def gather_hand(slot):
         for d in range(1, NF):
             fetch_copy(gathered[slot], slot, d).wait_recv()
-            if pair:
+            if halved(slot):
                 hand_copy(gathered[slot], slot, d).start()
 
     def gather_finish(slot):
-        if pair:
+        if halved(slot):
             for d in range(1, NF):
                 hand_copy(gathered[slot], slot, d).wait_recv()
 
@@ -475,49 +482,89 @@
 
         lax.fori_loop(0, D // 128, tile, 0)
 
+    def query_out_grad():
+        def tile(i, carry):
+            columns = pl.ds(pl.multiple_of(i * 128, 128), 128)
+            query = mm(tok[:, :, columns].reshape(R, 128), qb[:, :, 0:QW].reshape(R, QW), TN)
+            out = mm(ag3[:, :, :, columns].reshape(R, 128), att[...].reshape(R, 256), TN)
+            sources[1][columns, 0:128] = query[:, 0:128].astype(BF16)
+            sources[1][columns, 128:256] = (query[:, 128:256] + out[:, 0:128]).astype(BF16)
+            sources[1][columns, 256:384] = out[:, 128:256].astype(BF16)
+            return carry
+
+        lax.fori_loop(0, D // 128, tile, 0)
+
+    def block_rows(slot, block):
+        return half_rows(block, x) if two_level(slot) else own_rows(block)
+
+    def relayed(slot):
+        return NF == 4 and slot in RELAYED
+
+    z_near = z + 1 - 2 * (z % 2)
+    z_far = (z + 2) % NF
+
     def reduce_copy(slot, d):
         to = (z + d) % NF
-        rows = half_rows(to, x) if two_level(slot) else own_rows(to)
+        block = to
+        if relayed(slot):
+            to = z_far if d == 3 else z_near
+            block = (z_near + 2) % NF if d == 1 else to
         return remote(
-            sources[slot].at[rows, :], landings[slot].at[d - 1],
+            sources[slot].at[block_rows(slot, block), :], landings[slot].at[d - 1],
             gr_ss.at[slot, d - 1], gr_rs.at[slot, d - 1], "fsdp", to,
         )
 
+    def reduce_relay(slot):
+        if not relayed(slot):
+            return
+        reduce_copy(slot, 1).wait_recv()
+        rows = block_rows(slot, z_far)
+        sources[slot][rows, :] = (
+            sources[slot][rows, :].astype(F32) + landings[slot][0].astype(F32)
+        ).astype(BF16)
+        reduce_copy(slot, 3).start()
+
     def two_level(slot):
-        return pair and slot in (2, 3)
+        return pair and slot in SUM_HALVES
 
     def meet_copy(slot, block):
         return remote(
-            sources[slot].at[half_rows(block, 1 - x), :], meets[slot - 2].at[block],
-            h_ss.at[slot - 2, block], h_rs.at[slot - 2, block], "context", 1 - x,
-        )
+            sources[slot].at[half_rows(block, 1 - x), :], meets[SUM_HALVES.index(slot)].at[block],
+            h_ss.at[SUM_HALVES.index(slot), block], h_rs.at[SUM_HALVES.index(slot), block], "context", 1 - x,
+        )
+
+    def send_order(slot):
+        if relayed(slot):
+            return ((z_near + 2) % NF, z_near, z_far, z)
+        return [(z + d) % NF for d in range(1, NF + 1)]
+
+    def starts_now(slot, d):
+        return d < NF - 1 if relayed(slot) else d < NF
 
     def reduce_start(slot):
-        for d in range(1, NF):
+        for d, block in enumerate(send_order(slot), 1):
             if two_level(slot):
-                meet_copy(slot, (z + d) % NF).start()
-            else:
+                meet_copy(slot, block).start()
+            elif starts_now(slot, d):
                 reduce_copy(slot, d).start()
-        if two_level(slot):
-            meet_copy(slot, z).start()
 
     def reduce_meet(slot):
         if not two_level(slot):
             return
-        for d in range(1, NF + 1):
-            block = (z + d) % NF
+        for d, block in enumerate(send_order(slot), 1):
             meet_copy(slot, block).wait_recv()
             rows = half_rows(block, x)
             sources[slot][rows, :] = (
-                sources[slot][rows, :].astype(F32) + meets[slot - 2][block].astype(F32)
+                sources[slot][rows, :].astype(F32)
+                + meets[SUM_HALVES.index(slot)][block].astype(F32)
             ).astype(BF16)
-            if d < NF:
+            if starts_now(slot, d):
                 reduce_copy(slot, d).start()
 
     def reduce_middle(slot):
-        rows = half_rows(z, x) if two_level(slot) else own_rows(z)
+        rows = block_rows(slot, z)
         total = sources[slot][rows, :].astype(F32)
-        for d in range(1, NF):
+        for d in range(2 if relayed(slot) else 1, NF):
             reduce_copy(slot, d).wait_recv()
             total = total + landings[slot][d - 1].astype(F32)
         sources[slot][rows, :] = total.astype(BF16)
@@ -532,7 +579,7 @@
         place = pl.ds(pl.multiple_of(x * HB, HB), HB)
         return remote(
             sources[slot].at[half_rows(z, x), :], own_out[slot].at[place, :],
-            l_ss.at[slot - 2], l_rs.at[slot - 2], "context", 1 - x,
+            l_ss.at[SUM_HALVES.index(slot)], l_rs.at[SUM_HALVES.index(slot)], "context", 1 - x,
         )
 
     def cross_copy(slot, d):
@@ -624,9 +671,7 @@
             kvg_ss.at[d - 1, s], kvg_rs.at[d - 1, s], "context", (x + NC - d) % NC,
         )
 
-    def attend_back(s):
-        dqt[...] = jnp.zeros(dqt.shape, F32)
-
+    def back_block(s):
         def block(d):
             j = (x + NC - d) % NC
             doc_bias(j, s)
@@ -645,7 +690,7 @@
                 grads = (probs * (grad_probs - dlt[s, row, :])).astype(BF16)
                 dk[...] += mm(grads, keep(q_ref[s], key_mask), NN)
                 rows = pl.ds(pl.multiple_of(h * HD, HD), HD)
-                dqt[rows, :] += mm(vt[rows, :], grads, NN)
+                dqt[s, rows, :] += mm(vt[rows, :], grads, NN)
                 return inner
 
             lax.fori_loop(0, H, head, 0)
@@ -653,6 +698,12 @@
             second = dk[:, 128:256] * scale + dv[:, 0:128]
             return first, second, dv[:, 128:256]
 
+        return block
+
+    def attend_far(s):
+        dqt[s] = jnp.zeros(dqt.shape[1:], F32)
+        block = back_block(s)
+
         def far(d, carry):
             parts = block(d)
             if NC - 1 > KS:
@@ -668,10 +719,12 @@
 
         if NC > 1:
             lax.fori_loop(1, NC, far, 0)
-        parts = block(0)
+
+    def attend_near(s):
+        parts = back_block(s)(0)
         for k in range(3):
             kv_own[s, :, k * 128 : (k + 1) * 128] = parts[k].astype(BF16)
-        grad = jnp.transpose(dqt[...]) * scale
+        grad = jnp.transpose(dqt[s]) * scale
         q0, q1 = rotate_pair(grad, slice(0, T), -1.0)
         qb[s, :, 0:128] = q0.astype(BF16)
         qb[s, :, 128:256] = q1.astype(BF16)
@@ -704,7 +757,7 @@
     def input_copy(s):
         return pltpu.make_async_copy(n1.at[s], input_grad.at[s], loc_sem.at[1 + s])
 
-    seqs = range(S)
+    seqs = list(range(S))
     R = S * T
 
     for s in seqs:
@@ -752,36 +805,41 @@
         rs_produce(2, s, gate_product)
         if s > 0:
             rs_middle(2, s - 1)
+    weight_grad(
+        sources[2], lambda c: ag1[:, :, :, c].reshape(R, 128), gb[:, :, 0:F].reshape(R, F)
+    )
+    reduce_start(2)
     rs_middle(2, S - 1)
+    weight_grad(
+        sources[4], lambda c: ag1[:, :, :, c].reshape(R, 128), gb[:, :, F : 2 * F].reshape(R, F)
+    )
+    reduce_start(4)
+    for s in seqs[:-1]:
+        first_norm_back(s)
     weight_grad(sources[3], lambda c: ag2[:, :, :, c].reshape(R, 128), hid[...].reshape(R, F))
     reduce_start(3)
-    for s in seqs:
-        first_norm_back(s)
+    first_norm_back(S - 1)
     norm_start(0)
-    weight_grad(
-        sources[2], lambda c: ag1[:, :, :, c].reshape(R, 128), gb[...].reshape(R, 2 * F)
-    )
-    reduce_start(2)
+    reduce_meet(2)
     for s in seqs:
         ag_middle(2, ag3, s)
-    reduce_meet(3)
     for s in seqs:
         ag_finish(2, ag3, s)
         attended_back(s)
+        attend_far(s)
         if s == 0:
             nsum_c[x] = norm_total(0)
             norm_start(1)
-        attend_back(s)
-    reduce_meet(2)
+            reduce_relay(2)
+    reduce_meet(4)
+    reduce_relay(3)
+    for s in seqs:
+        attend_near(s)
     nsum_f[z] = norm_total(1)
     norm_start(2)
-    weight_grad(
-        sources[4], lambda c: tok[:, :, c].reshape(R, 128), qb[:, :, 0:QW].reshape(R, QW)
-    )
-    reduce_start(4)
-    weight_grad(sources[1], lambda c: ag3[:, :, :, c].reshape(R, 128), att[...].reshape(R, 256))
+    query_out_grad()
     reduce_start(1)
-    reduce_middle(3)
+    reduce_relay(4)
     for s in seqs:
         keys_back(s)
         if s == S - 1:
@@ -793,15 +851,19 @@
         rs_produce(3, s, input_product)
         if s > 0:
             rs_middle(3, s - 1)
+        else:
+            reduce_relay(1)
     rs_middle(3, S - 1)
+    reduce_middle(2)
     norm_out[...] = norm_total(2)
-    reduce_middle(2)
+    reduce_middle(3)
     reduce_middle(4)
-    reduce_middle(1)
     for s in seqs:
         input_out(s)
+    reduce_middle(1)
+    reduce_relay(0)
     reduce_middle(0)
-    for slot in (3, 2, 4, 1, 0):
+    for slot in (2, 4, 3, 1, 0):
         reduce_finish(slot)
 
     for s in seqs:
@@ -810,7 +872,7 @@
     for slot in range(4):
         for d in range(1, NF):
             fetch_copy(gathered[slot], slot, d).wait_send()
-            if pair:
+            if halved(slot):
                 hand_copy(gathered[slot], slot, d).wait_send()
     for s in seqs:
         for d in range(1, NC):
@@ -859,9 +921,9 @@
             (moments_in[2 * k].at[0], states[k].at[0]),
             (moments_in[2 * k + 1].at[0], states[k].at[1]),
         ]
-        for slot in ((0, 4) if k == 0 else (k,)):
+        for slot in ((2, 4) if k == 2 else (k,)):
             pairs.append((own_in[slot], own_g[slot]))
-            if not (pair and slot in (2, 3)):
+            if not (pair and slot in SUM_HALVES):
                 pairs.append((cross_in[slot], cross_g[slot]))
         return [
             pltpu.make_async_copy(src, dst, in_sem.at[k, i]) for i, (src, dst) in enumerate(pairs)
@@ -934,7 +996,7 @@
     def summed(slot):
         own = own_g[slot][...].astype(F32)
         if pair:
-            return own if slot in (2, 3) else own + cross_g[slot][0].astype(F32)
+            return own if slot in SUM_HALVES else own + cross_g[slot][0].astype(F32)
         total = jnp.zeros_like(own)
         for i in range(NC):
             other = cross_g[slot][jnp.maximum((x - i + NC) % NC, 1) - 1].astype(F32)
@@ -946,11 +1008,11 @@
             c.wait()
         total = summed(k)
         if k == 0:
-            parts = [summed(4)[:, 0:C], total[:, 0:C], total[:, C : 2 * C]]
+            parts = [summed(1)[:, 0:C], total[:, 0:C], total[:, C : 2 * C]]
         elif k == 1:
-            parts = [jnp.transpose(total)[HD : HD + C, :]]
+            parts = [jnp.transpose(total)[C : 2 * C, :]]
         elif k == 2:
-            parts = [total[:, 0:F], total[:, F : 2 * F]]
+            parts = [total, summed(4)]
         else:
             parts = [total]
         mine = owner[0:1, k : k + 1] == x
@@ -1024,7 +1086,7 @@
     VM = pltpu.VMEM
     DMA = pltpu.SemaphoreType.DMA
     NX = max(NC - 1, 1)
-    grad_columns = (KW, 256, 2 * F, F, 256)
+    grad_columns = (KW, KW, F, F, F)
     scratch = [
         VM((D, W), BF16), VM((D, 256), BF16), VM((D, 2 * F), BF16), VM((D, F), BF16),
         VM((NC, S, T), jnp.int32), VM((S, T, 256), BF16), VM((NC, S, T, KW), BF16),
@@ -1034,17 +1096,17 @@
         VM((S, 4, TS, D), BF16), VM((S, 4, TS, D), BF16), VM((S, 4, TS, D), BF16),
         VM((S, T, F), BF16), VM((S, T, 2 * F), BF16),
         VM((S, TS, D), F32), VM((S, TS, D), F32), VM((S, TS, 128), F32),
-        VM((S, T, 256), BF16), VM((S, 8, T), F32),
+        VM((S, T, 256), BF16), VM((S, 8, T), F32), VM((S, 256, T), F32),
         VM((T, 256), F32), VM((T, 256), F32), VM((min(NX, 2), S, T, KW), BF16), VM((NX, S, T, KW), BF16),
         VM((S, T, KW), BF16), VM((S, T, W), BF16),
         *(VM((D, columns), BF16) for columns in grad_columns),
         *(
-            VM((NF - 1, DB // 2 if NC == 2 and slot in (2, 3) else DB, grad_columns[slot]), BF16)
+            VM((NF - 1, DB // 2 if NC == 2 and slot in SUM_HALVES else DB, grad_columns[slot]), BF16)
             for slot in range(5)
         ),
         *(
-            VM((NF, DB // 2, columns) if NC == 2 else (1, 16, 128), BF16)
-            for columns in grad_columns[2:4]
+            VM((NF, DB // 2, grad_columns[slot]) if NC == 2 else (1, 16, 128), BF16)
+            for slot in SUM_HALVES
         ),
         VM((NT4, 8, D), F32), VM((NC, 8, D), F32), VM((NF, 8, D), F32), VM((S, TS, D), BF16),
         DMA((4, NF - 1)), DMA((4, NF - 1)), DMA((S, NX)), DMA((S, NX)), DMA((NX,)), DMA((NX,)),

time: 249 us -> 232 us (0.932)
  the two profiles are of different devices: /device:TPU:26 before, /device:TPU:8 now
where the time goes in v4:
time: 232 us; the launch traced here: 229 us
  Pallas kernels  224 us (97%)
    pallas_call x1, Pallas kernels, run_layer(): pl.pallas_call(functools.partial(layer_kernel, dims), out_shape=outs, in_...  210 us
    pallas_call x1, Pallas kernels, run_layer(): pl.pallas_call(functools.partial(finish_kernel, dims), out_shape=out_shap...  14.3 us

profile of v4, /device:TPU:8, one launch (start us, length us, event | category | flops | bytes accessed | tf_op | source)
XLA Modules:
  0.0 228.7 jit_solution(9510428773815918214)
XLA Ops:
  0.7 1.0 fusion
  1.7 1.3 pad_maximum_fusion
  2.9 209.8 %layer.1 = (bf16[2,128,768]{2,1,0:T(8,128)(2,1)}, f32[2,128,768]{2,1,0:T(8,128)}, bf16[192,384]{1,0:T(8,128)(2,1)}, bf16[192,384]{1,0:T(8,128)(2,1)}, bf16[192,7...) custom-call(bf16[2,512,768]{2,1,0:T(8,128)(2,1)} %refs_0_.1, ...), custom_call_target="tpu_custom_call" | custom-call | tf_op jit(solution)/shard_map/layer/pallas_call | solution.py:1143
  212.8 14.3 %finish.1 = (bf16[2,128,768]{2,1,0:T(8,128)(2,1)}, f32[2,128,768]{2,1,0:T(8,128)}, f32[3,192,192]{2,1,0:T(8,128)}, f32[192,192]{1,0:T(8,128)}, f32[192,2,768]{2,...) custom-call(s32[1,4]{1,0:T(1,128)} %bitcast.25, ...), custom_call_target="tpu_custom_call" | custom-call | tf_op jit(solution)/shard_map/finish/pallas_call | solution.py:1178
  227.0 1.2 bitcast_dynamic-update-slice_fusion
  (2 shorter events, 0.0 us)
